TPU v7x, 128 devices: a whole 4x4x4 slice. The times are simulated.
128 devices in a mesh: row: 2 (over x_lo), col: 4 (over y), layer: 16 (over z, x_hi, core).
Axes of the slice: x: 4 (x_hi: 2, x_lo: 2; x = x_hi * 2 + x_lo), y: 4, z: 4, core: 2. Of those that a mesh axis runs over, the one named last changes fastest.
Arguments:
- object_field: float32 [2, 512, 1024], P(None, 'row', 'col'), may hold values from -6 to 6
- probe_modes: float32 [2, 4, 256, 256], replicated, may hold values from -6 to 6
- amplitudes: float32 [128, 256, 256], P(('row', 'col', 'layer')), may hold values from 0 to 4
- offsets: int32 [128, 2], P(('row', 'col', 'layer')), may hold values from 0 to 768, as said below
Outputs:
- new_object: float32 [2, 512, 1024], P(None, 'row', 'col')
Inputs may be any that keep to these rules, and one draw needn't show every extreme that they name: `offsets`: every patch lies inside the 512 x 1024 object. A position held by the device at tile (r, c) has its corner inside that tile: rows r * 256 to (r + 1) * 256 - 1 and columns c * 256 to (c + 1) * 256 - 1. On a device whose tile row is not the last, its first position's patch reaches into the next tile row.
All inputs are finite; a program needn't handle non-finite values.
Results may differ from a plain program's by a relative error of at most 0.0001.
Values sent between devices are 32-bit elements; how exact they have to be, the bound alone decides.
A program may use at most 64 MiB of HBM per device.

v0:
```python
import functools
import math

import jax
import jax.numpy as jnp
import numpy as np
from jax import lax
from jax.experimental import pallas as pl
from jax.experimental.pallas import tpu as pltpu
from jax.sharding import PartitionSpec as P

SOFTEN = 0.05
DAMPING = 0.5
MODES = 4
SIDE = 256
HALF = 128
QUART = 64
F32 = jnp.float32
BF16 = jnp.bfloat16
VMEM_SPEC = pl.BlockSpec(memory_space=pltpu.VMEM)
SMEM_SPEC = pl.BlockSpec(memory_space=pltpu.SMEM)
ANY_SPEC = pl.BlockSpec(memory_space=pl.ANY)


def remote(src, dst, send, recv, device):
    return pltpu.make_async_remote_copy(
        src_ref=src,
        dst_ref=dst,
        send_sem=send,
        recv_sem=recv,
        device_id=device,
        device_id_type=pl.DeviceIdType.MESH,
    )


class Place:
    def __init__(self):
        self.row = lax.axis_index("row")
        self.col = lax.axis_index("col")
        layer = lax.axis_index("layer")
        self.layer = layer
        self.z = layer // 4
        self.xh = (layer // 2) % 2
        self.core = layer % 2
        self.partner = self.at(xh=self.xh, core=1 - self.core)
        self.far_x = self.at(xh=1 - self.xh)
        self.cross_xh = (self.xh + self.core) % 2
        self.cross = {"row": 1 - self.row, "layer": self.z * 4 + self.cross_xh * 2 + self.core}
        self.left = {"col": (self.col + 3) % 4}
        self.right = {"col": (self.col + 1) % 4}

    def at(self, z=None, xh=None, core=None):
        z = self.z if z is None else z
        xh = self.xh if xh is None else xh
        core = self.core if core is None else core
        return {"layer": z * 4 + xh * 2 + core}

    def z_peer(self, step):
        return self.at(z=(self.z + step) % 4)

    def meet(self):
        barrier = pltpu.get_barrier_semaphore()
        others = [self.partner, self.far_x, self.cross, self.left, self.right]
        others += [self.z_peer(step) for step in (1, 2, 3)]
        for other in others:
            pl.semaphore_signal(barrier, inc=1, device_id=other, device_id_type=pl.DeviceIdType.MESH)
        pl.semaphore_wait(barrier, len(others))


def rows_of(part, base=0):
    return pl.ds(pl.multiple_of(base + part * QUART, QUART), QUART)


def halo_kernel(
    offsets, obj, ext, spots,
    local_sem, right_send, right_recv, low_send, low_recv, diag_send, diag_recv,
    pair_send, pair_recv, spot_send, spot_recv,
):
    me = Place()
    core = me.core
    loads = []
    for plane in range(2):
        load = pltpu.make_async_copy(obj.at[plane], ext.at[0, plane, pl.ds(0, SIDE)], local_sem.at[plane])
        load.start()
        loads.append(load)
    lanes = lax.broadcasted_iota(jnp.int32, (1, 1, 128), 2)
    line = jnp.where(lanes == 0, offsets[0, 0], jnp.where(lanes == 1, offsets[0, 1], 0))
    spots[pl.ds(me.layer, 1)] = line
    me.meet()
    for load in loads:
        load.wait()

    has_right = me.col < 3
    has_left = me.col > 0
    top = me.row == 0
    bottom = me.row == 1

    def right_copy(part):
        return remote(ext.at[0, core, rows_of(part)], ext.at[1, core, rows_of(part)],
                      right_send.at[part], right_recv.at[part], me.left)

    def low_copy(part):
        return remote(ext.at[0, core, rows_of(part)], ext.at[0, core, rows_of(part, SIDE)],
                      low_send.at[part], low_recv.at[part], me.cross)

    def diag_copy(part):
        return remote(ext.at[1, core, rows_of(part)], ext.at[1, core, rows_of(part, SIDE)],
                      diag_send.at[part], diag_recv.at[part], me.cross)

    def pair_copy(kind, part):
        side, base = ((1, 0), (0, SIDE), (1, SIDE))[kind]
        where = ext.at[side, core, rows_of(part, base)]
        return remote(where, where, pair_send.at[kind, part], pair_recv.at[kind, part], me.partner)

    @pl.when(has_left)
    def _():
        for part in range(4):
            right_copy(part).start()

    @pl.when(bottom)
    def _():
        for part in range(4):
            low_copy(part).start()

    def spot_copy(step):
        if step == 0:
            where = pl.ds(me.layer, 1)
            return remote(spots.at[where], spots.at[where], spot_send.at[0], spot_recv.at[0], me.partner)
        if step == 1:
            where = pl.ds(me.z * 4 + me.xh * 2, 2)
            return remote(spots.at[where], spots.at[where], spot_send.at[1], spot_recv.at[1], me.far_x)
        if step < 5:
            where = pl.ds(me.z * 4, 4)
            return remote(spots.at[where], spots.at[where], spot_send.at[step], spot_recv.at[step],
                          me.z_peer(step - 1))
        if step == 5:
            return remote(spots.at[pl.ds(0, 16)], spots.at[pl.ds(16, 16)], spot_send.at[5], spot_recv.at[5], me.right)
        return remote(spots.at[pl.ds(0, 32)], spots.at[pl.ds(32, 32)], spot_send.at[6], spot_recv.at[6], me.cross)

    def spots_go(stage):
        if stage == 0:
            spot_copy(0).start()
        elif stage == 1:
            spot_copy(0).wait_recv()
            spot_copy(1).start()
        elif stage == 2:
            spot_copy(1).wait_recv()
            for step in (2, 3, 4):
                spot_copy(step).start()
        elif stage == 3:
            for step in (2, 3, 4):
                spot_copy(step).wait_recv()

            @pl.when(has_right)
            def _():
                spot_copy(5).start()
        elif stage == 4:
            @pl.when(has_left)
            def _():
                spot_copy(5).wait_recv()

            @pl.when(top)
            def _():
                spot_copy(6).start()
        else:
            @pl.when(bottom)
            def _():
                spot_copy(6).wait_recv()

    spots_go(0)
    for part in range(4):
        @pl.when(has_right)
        def _():
            right_copy(part).wait_recv()

            @pl.when(bottom)
            def _():
                diag_copy(part).start()

            pair_copy(0, part).start()

        @pl.when(top)
        def _():
            low_copy(part).wait_recv()
            pair_copy(1, part).start()

        spots_go(part + 1)

    @pl.when(jnp.logical_and(top, has_right))
    def _():
        for part in range(4):
            diag_copy(part).wait_recv()
            pair_copy(2, part).start()

    spots_go(5)

    @pl.when(has_left)
    def _():
        for part in range(4):
            right_copy(part).wait_send()

    @pl.when(bottom)
    def _():
        for part in range(4):
            low_copy(part).wait_send()

            @pl.when(has_right)
            def _():
                diag_copy(part).wait_send()

    @pl.when(has_right)
    def _():
        for part in range(4):
            pair_copy(0, part).wait_send()
            other_pair(ext, pair_send, pair_recv, me, 0, part).wait_recv()

    @pl.when(top)
    def _():
        for part in range(4):
            pair_copy(1, part).wait_send()
            other_pair(ext, pair_send, pair_recv, me, 1, part).wait_recv()

            @pl.when(has_right)
            def _():
                pair_copy(2, part).wait_send()
                other_pair(ext, pair_send, pair_recv, me, 2, part).wait_recv()

    for step in range(5):
        spot_copy(step).wait_send()

    @pl.when(has_right)
    def _():
        spot_copy(5).wait_send()

    @pl.when(top)
    def _():
        spot_copy(6).wait_send()


def other_pair(ext, pair_send, pair_recv, me, kind, part):
    side, base = ((1, 0), (0, SIDE), (1, SIDE))[kind]
    where = ext.at[side, 1 - me.core, rows_of(part, base)]
    return remote(where, where, pair_send.at[kind, part], pair_recv.at[kind, part], me.partner)


def halo(offsets, obj):
    sems = pltpu.SemaphoreType.DMA
    return pl.pallas_call(
        halo_kernel,
        out_shape=(
            jax.ShapeDtypeStruct((2, 2, 2 * SIDE, SIDE), F32),
            jax.ShapeDtypeStruct((64, 1, 128), jnp.int32),
        ),
        in_specs=[SMEM_SPEC, ANY_SPEC],
        out_specs=(VMEM_SPEC, VMEM_SPEC),
        scratch_shapes=[
            sems((2,)), sems((4,)), sems((4,)), sems((4,)), sems((4,)), sems((4,)), sems((4,)),
            sems((3, 4)), sems((3, 4)), sems((7,)), sems((7,)),
        ],
        compiler_params=pltpu.CompilerParams(collective_id=0, has_side_effects=True),
        name="halo",
    )(offsets, obj)


def tables():
    steps = np.arange(HALF)
    found = []
    for odd in (0, 1):
        phase = (steps[:, None] * (2 * steps[None, :] + odd)) % SIDE
        angle = phase * (2.0 * math.pi / SIDE)
        real, imag = np.cos(angle) / 16.0, -np.sin(angle) / 16.0
        full = np.block([[real, imag], [-imag, real]]).astype(np.float32)
        for table in (full, np.ascontiguousarray(full.T)):
            high = table.astype(jnp.bfloat16)
            low = (table - high.astype(np.float32)).astype(jnp.bfloat16)
            found += [high, low]
    order = np.zeros((SIDE, SIDE), np.float32)
    order[2 * steps, steps] = 1.0
    order[2 * steps + 1, HALF + steps] = 1.0
    found += [order.astype(jnp.bfloat16), np.ascontiguousarray(order.T).astype(jnp.bfloat16)]
    return np.stack(found)


EVEN, EVEN_T, ODD, ODD_T, ORDER, ORDER_T = 0, 2, 4, 6, 8, 9


def dot(left, right):
    return jnp.dot(left, right, preferred_element_type=F32)


def split(value):
    high = value.astype(BF16)
    return high, (value - high.astype(F32)).astype(BF16)


def on_lanes(value, tabs, which):
    high, low = split(value)
    return dot(high, tabs[which]) + dot(low, tabs[which]) + dot(high, tabs[which + 1])


def on_rows(value, tabs, which):
    high, low = split(value)
    return dot(tabs[which], high) + dot(tabs[which], low) + dot(tabs[which + 1], high)


def side_by_side(left, right):
    return jnp.concatenate([left, right], axis=1)


def on_top(upper, lower):
    return jnp.concatenate([upper, lower], axis=0)


def forward(mode, probe, patch, tabs, far):
    pr, pi = probe[0, mode], probe[1, mode]
    tr, ti = patch[0], patch[1]
    er = pr * tr - pi * ti
    ei = pr * ti + pi * tr
    even = side_by_side(er[:, :HALF] + er[:, HALF:], ei[:, :HALF] + ei[:, HALF:])
    odd = side_by_side(er[:, :HALF] - er[:, HALF:], ei[:, :HALF] - ei[:, HALF:])
    ye = on_lanes(even, tabs, EVEN)
    yo = on_lanes(odd, tabs, ODD)
    for parity, which in ((0, EVEN_T), (1, ODD_T)):
        if parity == 0:
            se, so = ye[:HALF] + ye[HALF:], yo[:HALF] + yo[HALF:]
        else:
            se, so = ye[:HALF] - ye[HALF:], yo[:HALF] - yo[HALF:]
        stack = on_top(side_by_side(se[:, :HALF], so[:, :HALF]), side_by_side(se[:, HALF:], so[:, HALF:]))
        far[mode, parity] = on_rows(stack, tabs, which)


def backward(mode, probe, ratio, tabs, far, block):
    sums = []
    for parity, which in ((0, EVEN), (1, ODD)):
        scale = ratio[parity]
        sums.append(on_rows(far[mode, parity] * on_top(scale, scale), tabs, which))
    upper, lower = sums[0] + sums[1], sums[0] - sums[1]
    even = on_top(side_by_side(upper[:HALF, :HALF], upper[HALF:, :HALF]),
                  side_by_side(lower[:HALF, :HALF], lower[HALF:, :HALF]))
    odd = on_top(side_by_side(upper[:HALF, HALF:], upper[HALF:, HALF:]),
                 side_by_side(lower[:HALF, HALF:], lower[HALF:, HALF:]))
    pe = on_lanes(even, tabs, EVEN_T)
    po = on_lanes(odd, tabs, ODD_T)
    first, second = pe + po, pe - po
    nr = side_by_side(first[:, :HALF], second[:, :HALF])
    ni = side_by_side(first[:, HALF:], second[:, HALF:])
    pr, pi = probe[0, mode], probe[1, mode]
    cr = pr * nr + pi * ni
    ci = pr * ni - pi * nr
    if mode == 0:
        block[0] = cr
        block[1] = ci
    else:
        block[0] = block[0] + cr
        block[1] = block[1] + ci


def rows_from(ref, start, count):
    near = pl.multiple_of(start // 8 * 8, 8)
    wide = ref[pl.ds(near, count + 8), :]
    return pltpu.roll(wide, lax.rem(count + 8 - (start - near), count + 8), 0)[:count]


def local_kernel(
    place, offsets, spots, ext, probe, amp, tabs, frame, share, patch, far, ratio, block, padded
):
    row, col, z = place[0], place[1], place[2]
    row_at = offsets[0, 0] - row * SIDE
    col_at = offsets[0, 1] - col * SIDE
    lanes = lax.broadcasted_iota(jnp.int32, (SIDE, SIDE), 1)
    back = lax.rem(SIDE - col_at, SIDE)
    for plane in range(2):
        here = pltpu.roll(rows_from(ext.at[0, plane], row_at, SIDE), back, 1)
        there = pltpu.roll(rows_from(ext.at[1, plane], row_at, SIDE), back, 1)
        patch[plane] = jnp.where(lanes < SIDE - col_at, here, there)

    rest = amp[...]
    total = None
    for _ in range(3):
        piece = rest.astype(BF16)
        rest = rest - piece.astype(F32)
        moved = dot(dot(tabs[ORDER_T], piece).astype(BF16), tabs[ORDER])
        total = moved if total is None else total + moved
    ratio[0] = total[:HALF]
    ratio[1] = total[HALF:]

    for mode in range(MODES):
        forward(mode, probe, patch, tabs, far)
    for parity in range(2):
        seen = None
        for mode in range(MODES):
            re, im = far[mode, parity, :HALF], far[mode, parity, HALF:]
            term = re * re + im * im
            seen = term if seen is None else seen + term
        ratio[parity] = ratio[parity] / (jnp.sqrt(seen) + SOFTEN)
    for mode in range(MODES):
        backward(mode, probe, ratio, tabs, far, block)

    frame[...] = jnp.zeros_like(frame)
    for plane in range(2):
        turned = pltpu.roll(block[plane], col_at, 1)
        near = pl.multiple_of(row_at // 8 * 8, 8)
        for side, kept in ((0, lanes >= col_at), (1, lanes < col_at)):
            value = on_top(jnp.where(kept, turned, 0.0), jnp.zeros((8, SIDE), F32))
            frame[side, plane, pl.ds(near, SIDE + 8), :] = pltpu.roll(value, row_at - near, 0)

    padded[...] = jnp.zeros_like(padded)
    power = None
    for mode in range(MODES):
        term = probe[0, mode] * probe[0, mode] + probe[1, mode] * probe[1, mode]
        power = term if power is None else power + term
    padded[pl.ds(SIDE, SIDE), :] = power
    share[...] = jnp.zeros_like(share)
    first = row * SIDE + z * QUART
    narrow = lax.broadcasted_iota(jnp.int32, (QUART, SIDE), 1)

    def add_spot(index, carry):
        up = index // 32
        left = (index // 16) % 2
        known = jnp.logical_and(row >= up, col >= left)
        spot_row = spots[index, 0, 0]
        spot_col = spots[index, 0, 1] - (col - left) * SIDE
        start = jnp.where(known, first - spot_row + SIDE, 0)
        turn = jnp.where(known, spot_col, 0)
        turned = pltpu.roll(rows_from(padded, start, QUART), turn, 1)
        kept = jnp.where(left == 0, narrow, SIDE - 1 - narrow) >= jnp.where(left == 0, turn, SIDE - turn)
        share[...] = share[...] + jnp.where(kept, turned, 0.0)
        return carry

    lax.fori_loop(0, 64, add_spot, 0)


def local_work(place, offsets, spots, ext, probe, amp, tabs):
    return pl.pallas_call(
        local_kernel,
        out_shape=(
            jax.ShapeDtypeStruct((2, 2, 2 * SIDE, SIDE), F32),
            jax.ShapeDtypeStruct((QUART, SIDE), F32),
        ),
        in_specs=[SMEM_SPEC, SMEM_SPEC, SMEM_SPEC, VMEM_SPEC, VMEM_SPEC, VMEM_SPEC, VMEM_SPEC],
        out_specs=(VMEM_SPEC, VMEM_SPEC),
        scratch_shapes=[
            pltpu.VMEM((2, SIDE, SIDE), F32),
            pltpu.VMEM((MODES, 2, SIDE, SIDE), F32),
            pltpu.VMEM((2, HALF, SIDE), F32),
            pltpu.VMEM((2, SIDE, SIDE), F32),
            pltpu.VMEM((3 * SIDE, SIDE), F32),
        ],
        compiler_params=pltpu.CompilerParams(),
        name="local",
    )(place, offsets, spots, ext, probe, amp, tabs)


def gather_kernel(
    frame, share, obj, out,
    pair, low_sum, low_in, right_sum, right_in, total, z_in, x_out, x_in,
    pair_send, pair_recv, low_send, low_recv, right_send, right_recv,
    z_send, z_recv, x_send, x_recv, out_send, out_recv, twin_send, twin_recv,
):
    me = Place()
    core = me.core
    has_right = me.col < 3
    has_left = me.col > 0
    top = me.row == 0
    bottom = me.row == 1
    parts = [(me.z + 1 + step) % 4 for step in range(4)]

    def pair_copy(kind, step):
        where = rows_of(parts[step], SIDE * kind)
        return remote(frame.at[:, 1 - core, where], pair.at[:, where],
                      pair_send.at[kind, step], pair_recv.at[kind, step], me.partner)

    def low_copy(step):
        where = rows_of(parts[step])
        return remote(low_sum.at[:, where], low_in.at[:, where], low_send.at[step], low_recv.at[step], me.cross)

    def right_copy(step):
        where = rows_of(parts[step])
        return remote(right_sum.at[where], right_in.at[where], right_send.at[step], right_recv.at[step], me.right)

    def z_copy(step):
        return remote(total.at[rows_of(parts[step])], z_in.at[step], z_send.at[step], z_recv.at[step],
                      me.z_peer(step + 1))

    me.meet()
    for step in range(4):
        @pl.when(top)
        def _():
            pair_copy(1, step).start()

        pair_copy(0, step).start()

    for step in range(4):
        where = rows_of(parts[step])
        under = rows_of(parts[step], SIDE)

        @pl.when(top)
        def _():
            pair_copy(1, step).wait_recv()
            for side in range(2):
                low_sum[side, where] = frame[side, core, under] + pair[side, under]
            low_copy(step).start()

        pair_copy(0, step).wait_recv()
        total[where] = frame[0, core, where] + pair[0, where]
        right_sum[where] = frame[1, core, where] + pair[1, where]

        @pl.when(bottom)
        def _():
            low_copy(step).wait_recv()
            total[where] = total[where] + low_in[0, where]
            right_sum[where] = right_sum[where] + low_in[1, where]

        @pl.when(has_right)
        def _():
            right_copy(step).start()

    for step in range(4):
        where = rows_of(parts[step])

        @pl.when(has_left)
        def _():
            right_copy(step).wait_recv()
            total[where] = total[where] + right_in[where]

        if step < 3:
            z_copy(step).start()

    mine = rows_of(me.z)
    for step in range(3):
        z_copy(step).wait_recv()
    x_out[...] = total[mine] + z_in[0] + z_in[1] + z_in[2]
    x_copy = remote(x_out, x_in, x_send.at[0], x_recv.at[0], me.far_x)
    x_copy.start()
    x_copy.wait_recv()
    whole = x_out[...] + x_in[...]
    out[core, mine] = (whole + DAMPING * obj[core, mine]) / (share[...] + DAMPING)

    def out_copy(step):
        return remote(out.at[core, mine], out.at[core, mine], out_send.at[step], out_recv.at[step], me.z_peer(step + 1))

    def come_copy(step):
        where = out.at[core, rows_of((me.z + 3 - step) % 4)]
        return remote(where, where, out_send.at[step], out_recv.at[step], me.z_peer(step + 1))

    def twin_copy(step, plane):
        part = me.z if step == 3 else (me.z + 3 - step) % 4
        where = out.at[plane, rows_of(part)]
        return remote(where, where, twin_send.at[step], twin_recv.at[step], me.partner)

    for step in (1, 0, 2):
        out_copy(step).start()
    twin_copy(3, core).start()
    for step in (0, 2, 1):
        come_copy(step).wait_recv()
        twin_copy(step, core).start()
    for step in (3, 0, 2, 1):
        twin_copy(step, 1 - core).wait_recv()

    for step in range(4):
        pair_copy(0, step).wait_send()
        twin_copy(step, core).wait_send()

        @pl.when(top)
        def _():
            pair_copy(1, step).wait_send()
            low_copy(step).wait_send()

        @pl.when(has_right)
        def _():
            right_copy(step).wait_send()

        if step < 3:
            z_copy(step).wait_send()
            out_copy(step).wait_send()
    x_copy.wait_send()


def gather(frame, share, obj):
    sems = pltpu.SemaphoreType.DMA
    return pl.pallas_call(
        gather_kernel,
        out_shape=jax.ShapeDtypeStruct((2, SIDE, SIDE), F32),
        in_specs=[VMEM_SPEC] * 3,
        out_specs=VMEM_SPEC,
        scratch_shapes=[
            pltpu.VMEM((2, 2 * SIDE, SIDE), F32),
            pltpu.VMEM((2, SIDE, SIDE), F32),
            pltpu.VMEM((2, SIDE, SIDE), F32),
            pltpu.VMEM((SIDE, SIDE), F32),
            pltpu.VMEM((SIDE, SIDE), F32),
            pltpu.VMEM((SIDE, SIDE), F32),
            pltpu.VMEM((3, QUART, SIDE), F32),
            pltpu.VMEM((QUART, SIDE), F32),
            pltpu.VMEM((QUART, SIDE), F32),
            sems((2, 4)), sems((2, 4)), sems((4,)), sems((4,)), sems((4,)), sems((4,)),
            sems((3,)), sems((3,)), sems((1,)), sems((1,)), sems((3,)), sems((3,)), sems((4,)), sems((4,)),
        ],
        compiler_params=pltpu.CompilerParams(collective_id=1, has_side_effects=True),
        name="gather",
    )(frame, share, obj)


def body(object_field, probe_modes, amplitudes, offsets):
    ext, spots = halo(offsets, object_field)
    place = jnp.stack([lax.axis_index("row"), lax.axis_index("col"), lax.axis_index("layer") // 4]).astype(jnp.int32)
    frame, share = local_work(place, offsets, spots, ext, probe_modes, amplitudes[0], jnp.asarray(tables()))
    return gather(frame, share, object_field)


def solution(mesh):
    placed = (
        P(None, "row", "col"),
        P(),
        P(("row", "col", "layer"), None, None),
        P(("row", "col", "layer"), None),
    )
    return jax.shard_map(
        body, mesh=mesh, in_specs=placed, out_specs=P(None, "row", "col"), check_vma=False
    )
```

profile of v0, /device:TPU:3, one launch (start us, length us, event | category | flops | bytes accessed | tf_op | source)
XLA Modules:
  0.0 74.1 jit_solution(7587179957529592536)
XLA Ops:
  0.0 0.6 pad_add_fusion.place
  0.6 20.1 %halo.1 = (f32[2,2,512,256]{3,2,1,0:T(8,128)}, s32[64,1,128]{2,1,0:T(1,128)}) custom-call(s32[1,2]{1,0:T(1,128)} %offsets.3, f32[2,256,256]{2,1,0:T(8,128)} %obj.3), custom_call_target="tpu_custom_call" | custom-call | tf_op jit(solution)/shard_map/halo/pallas_call | solution.py:248
  20.7 18.4 %local.1 = (f32[2,2,512,256]{3,2,1,0:T(8,128)}, f32[64,256]{1,0:T(8,128)}) custom-call(s32[3]{0:T(128)} %pad_add_fusion.place, s32[1,2]{1,0:T(1,128)} %offsets.3, s32[64,1,128]{2,1,0:T(1,128)} %get-tuple-element.9.spots, f32[2,2,512,256]{3,2,1,0:T(8,128)} %get-tuple-element.10.ext, f32[2,4,256,256]{3,2,1,0:T(8,128)} %probe.1, f32[256,256]{1,0:T(8,128)} %bitcast.4, ...), custom_call_target="tpu_custom_call" | custom-call | tf_op jit(solution)/shard_map/local/pallas_call | solution.py:434
  39.1 33.2 %gather.1 = f32[2,256,256]{2,1,0:T(8,128)} custom-call(f32[2,2,512,256]{3,2,1,0:T(8,128)} %get-tuple-element.11.frame, f32[64,256]{1,0:T(8,128)} %get-tuple-element.12.share, f32[2,256,256]{2,1,0:T(8,128)} %obj.3), custom_call_target="tpu_custom_call" | custom-call | tf_op jit(solution)/shard_map/gather/pallas_call | solution.py:581
  72.3 1.9 %copy.7 = f32[2,256,256]{2,1,0:T(8,128)} copy(f32[2,256,256]{2,1,0:T(8,128)} %gather.1) | data formatting | bytes 1048576
where the time goes:
time: 74.3 us; the launch traced here: 74.1 us
  Pallas kernels  71.7 us (97%)
  local copies, waits for them, and re-layouts  1.87 us (3%)
    pallas_call x1, Pallas kernels, gather(): pl.pallas_call(gather_kernel, out_shape=jax.ShapeDtypeStruct((2, SIDE, SI...  33.2 us
    pallas_call x1, Pallas kernels, halo(): pl.pallas_call(halo_kernel, out_shape=(jax.ShapeDtypeStruct((2, 2, 2 * SI...  20.1 us
    pallas_call x1, Pallas kernels, local_work(): pl.pallas_call(local_kernel, out_shape=(jax.ShapeDtypeStruct((2, 2, 2 * S...  18.4 us
    unnamed x1, local copies, waits for them, and re-layouts  1.87 us

commit v1 on v0

v1 whole, which is shorter than its diff:
```python
import functools
import math

import jax
import jax.numpy as jnp
import numpy as np
from jax import lax
from jax.experimental import pallas as pl
from jax.experimental.pallas import tpu as pltpu
from jax.sharding import PartitionSpec as P

SOFTEN = 0.05
DAMPING = 0.5
MODES = 4
SIDE = 256
HALF = 128
QUART = 64
F32 = jnp.float32
BF16 = jnp.bfloat16
VMEM_SPEC = pl.BlockSpec(memory_space=pltpu.VMEM)
SMEM_SPEC = pl.BlockSpec(memory_space=pltpu.SMEM)
ANY_SPEC = pl.BlockSpec(memory_space=pl.ANY)


def remote(src, dst, send, recv, device):
    return pltpu.make_async_remote_copy(
        src_ref=src,
        dst_ref=dst,
        send_sem=send,
        recv_sem=recv,
        device_id=device,
        device_id_type=pl.DeviceIdType.MESH,
    )


class Place:
    def __init__(self):
        self.row = lax.axis_index("row")
        self.col = lax.axis_index("col")
        layer = lax.axis_index("layer")
        self.layer = layer
        self.z = layer // 4
        self.xh = (layer // 2) % 2
        self.core = layer % 2
        self.partner = self.at(xh=self.xh, core=1 - self.core)
        self.far_x = self.at(xh=1 - self.xh)
        self.cross_xh = (self.xh + self.core) % 2
        self.cross = {"row": 1 - self.row, "layer": self.z * 4 + self.cross_xh * 2 + self.core}
        self.left = {"col": (self.col + 3) % 4}
        self.right = {"col": (self.col + 1) % 4}

    def at(self, z=None, xh=None, core=None):
        z = self.z if z is None else z
        xh = self.xh if xh is None else xh
        core = self.core if core is None else core
        return {"layer": z * 4 + xh * 2 + core}

    def z_peer(self, step):
        return self.at(z=(self.z + step) % 4)

    def meet(self):
        barrier = pltpu.get_barrier_semaphore()
        others = [self.partner, self.far_x, self.cross, self.left, self.right]
        others += [self.z_peer(step) for step in (1, 2, 3)]
        for other in others:
            pl.semaphore_signal(barrier, inc=1, device_id=other, device_id_type=pl.DeviceIdType.MESH)
        pl.semaphore_wait(barrier, len(others))


def rows_of(part, base=0):
    return pl.ds(pl.multiple_of(base + part * QUART, QUART), QUART)


def groups_of(part, base=0):
    return pl.ds(base // 8 + part * (QUART // 8), QUART // 8)


def tables():
    steps = np.arange(HALF)
    found = []
    for odd in (0, 1):
        phase = (steps[:, None] * (2 * steps[None, :] + odd)) % SIDE
        angle = phase * (2.0 * math.pi / SIDE)
        real, imag = np.cos(angle) / 16.0, -np.sin(angle) / 16.0
        full = np.block([[real, imag], [-imag, real]]).astype(np.float32)
        for table in (full, np.ascontiguousarray(full.T)):
            high = table.astype(jnp.bfloat16)
            low = (table - high.astype(np.float32)).astype(jnp.bfloat16)
            found += [high, low]
    order = np.zeros((SIDE, SIDE), np.float32)
    order[2 * steps, steps] = 1.0
    order[2 * steps + 1, HALF + steps] = 1.0
    found += [order.astype(jnp.bfloat16), np.ascontiguousarray(order.T).astype(jnp.bfloat16)]
    return np.stack(found)


EVEN, EVEN_T, ODD, ODD_T, ORDER, ORDER_T = 0, 2, 4, 6, 8, 9


def dot(left, right):
    return jnp.dot(left, right, preferred_element_type=F32)


def split(value):
    high = value.astype(BF16)
    return high, (value - high.astype(F32)).astype(BF16)


def on_lanes(value, tabs, which):
    high, low = split(value)
    return dot(high, tabs[which]) + dot(low, tabs[which]) + dot(high, tabs[which + 1])


def on_rows(value, tabs, which):
    high, low = split(value)
    return dot(tabs[which], high) + dot(tabs[which], low) + dot(tabs[which + 1], high)


def side_by_side(left, right):
    return jnp.concatenate([left, right], axis=1)


def on_top(upper, lower):
    return jnp.concatenate([upper, lower], axis=0)


def halo(me, ext, spots, right_send, right_recv, low_send, low_recv, diag_send, diag_recv, pair_send, pair_recv,
         spot_send, spot_recv, meanwhile):
    core = me.core
    has_right = me.col < 3
    has_left = me.col > 0
    top = me.row == 0
    bottom = me.row == 1

    def right_copy(part):
        return remote(ext.at[0, core, groups_of(part)], ext.at[1, core, groups_of(part)],
                      right_send.at[part], right_recv.at[part], me.left)

    def low_copy(part):
        return remote(ext.at[0, core, groups_of(part)], ext.at[0, core, groups_of(part, SIDE)],
                      low_send.at[part], low_recv.at[part], me.cross)

    def diag_copy(part):
        return remote(ext.at[1, core, groups_of(part)], ext.at[1, core, groups_of(part, SIDE)],
                      diag_send.at[part], diag_recv.at[part], me.cross)

    def pair_copy(kind, part):
        side, base = ((1, 0), (0, SIDE), (1, SIDE))[kind]
        where = ext.at[side, core, groups_of(part, base)]
        return remote(where, where, pair_send.at[kind, part], pair_recv.at[kind, part], me.partner)

    @pl.when(has_left)
    def _():
        for part in range(4):
            right_copy(part).start()

    @pl.when(bottom)
    def _():
        for part in range(4):
            low_copy(part).start()

    def spot_copy(step):
        if step == 0:
            where = pl.ds(me.layer, 1)
            return remote(spots.at[where], spots.at[where], spot_send.at[0], spot_recv.at[0], me.partner)
        if step == 1:
            where = pl.ds(me.z * 4 + me.xh * 2, 2)
            return remote(spots.at[where], spots.at[where], spot_send.at[1], spot_recv.at[1], me.far_x)
        if step < 5:
            where = pl.ds(me.z * 4, 4)
            return remote(spots.at[where], spots.at[where], spot_send.at[step], spot_recv.at[step],
                          me.z_peer(step - 1))
        if step == 5:
            return remote(spots.at[pl.ds(0, 16)], spots.at[pl.ds(16, 16)], spot_send.at[5], spot_recv.at[5], me.right)
        return remote(spots.at[pl.ds(0, 32)], spots.at[pl.ds(32, 32)], spot_send.at[6], spot_recv.at[6], me.cross)

    def spots_go(stage):
        if stage == 0:
            spot_copy(0).start()
        elif stage == 1:
            spot_copy(0).wait_recv()
            spot_copy(1).start()
        elif stage == 2:
            spot_copy(1).wait_recv()
            for step in (2, 3, 4):
                spot_copy(step).start()
        elif stage == 3:
            for step in (2, 3, 4):
                spot_copy(step).wait_recv()

            @pl.when(has_right)
            def _():
                spot_copy(5).start()
        elif stage == 4:
            @pl.when(has_left)
            def _():
                spot_copy(5).wait_recv()

            @pl.when(top)
            def _():
                spot_copy(6).start()
        else:
            @pl.when(bottom)
            def _():
                spot_copy(6).wait_recv()

    spots_go(0)
    meanwhile()
    for part in range(4):
        @pl.when(has_right)
        def _():
            right_copy(part).wait_recv()

            @pl.when(bottom)
            def _():
                diag_copy(part).start()

            pair_copy(0, part).start()

        @pl.when(top)
        def _():
            low_copy(part).wait_recv()
            pair_copy(1, part).start()

        spots_go(part + 1)

    @pl.when(jnp.logical_and(top, has_right))
    def _():
        for part in range(4):
            diag_copy(part).wait_recv()
            pair_copy(2, part).start()

    spots_go(5)

    @pl.when(has_left)
    def _():
        for part in range(4):
            right_copy(part).wait_send()

    @pl.when(bottom)
    def _():
        for part in range(4):
            low_copy(part).wait_send()

            @pl.when(has_right)
            def _():
                diag_copy(part).wait_send()

    @pl.when(has_right)
    def _():
        for part in range(4):
            pair_copy(0, part).wait_send()
            other_pair(ext, pair_send, pair_recv, me, 0, part).wait_recv()

    @pl.when(top)
    def _():
        for part in range(4):
            pair_copy(1, part).wait_send()
            other_pair(ext, pair_send, pair_recv, me, 1, part).wait_recv()

            @pl.when(has_right)
            def _():
                pair_copy(2, part).wait_send()
                other_pair(ext, pair_send, pair_recv, me, 2, part).wait_recv()

    for step in range(5):
        spot_copy(step).wait_send()

    @pl.when(has_right)
    def _():
        spot_copy(5).wait_send()

    @pl.when(top)
    def _():
        spot_copy(6).wait_send()


def other_pair(ext, pair_send, pair_recv, me, kind, part):
    side, base = ((1, 0), (0, SIDE), (1, SIDE))[kind]
    where = ext.at[side, 1 - me.core, groups_of(part, base)]
    return remote(where, where, pair_send.at[kind, part], pair_recv.at[kind, part], me.partner)


def forward(mode, probe, patch, tabs, far):
    pr, pi = probe[0, mode], probe[1, mode]
    tr, ti = patch[0], patch[1]
    er = pr * tr - pi * ti
    ei = pr * ti + pi * tr
    even = side_by_side(er[:, :HALF] + er[:, HALF:], ei[:, :HALF] + ei[:, HALF:])
    odd = side_by_side(er[:, :HALF] - er[:, HALF:], ei[:, :HALF] - ei[:, HALF:])
    ye = on_lanes(even, tabs, EVEN)
    yo = on_lanes(odd, tabs, ODD)
    for parity, which in ((0, EVEN_T), (1, ODD_T)):
        if parity == 0:
            se, so = ye[:HALF] + ye[HALF:], yo[:HALF] + yo[HALF:]
        else:
            se, so = ye[:HALF] - ye[HALF:], yo[:HALF] - yo[HALF:]
        stack = on_top(side_by_side(se[:, :HALF], so[:, :HALF]), side_by_side(se[:, HALF:], so[:, HALF:]))
        far[mode, parity] = on_rows(stack, tabs, which)


def backward_rows(mode, ratio, tabs, far):
    sums = []
    for parity, which in ((0, EVEN), (1, ODD)):
        scale = ratio[parity]
        sums.append(on_rows(far[mode, parity] * on_top(scale, scale), tabs, which))
    far[mode, 0] = sums[0] + sums[1]
    far[mode, 1] = sums[0] - sums[1]


def backward_lanes(half, probe, tabs, far, block):
    even = [side_by_side(far[mode, half, :HALF, :HALF], far[mode, half, HALF:, :HALF]) for mode in range(MODES)]
    odd = [side_by_side(far[mode, half, :HALF, HALF:], far[mode, half, HALF:, HALF:]) for mode in range(MODES)]
    pe = on_lanes(jnp.concatenate(even, axis=0), tabs, EVEN_T)
    po = on_lanes(jnp.concatenate(odd, axis=0), tabs, ODD_T)
    first, second = pe + po, pe - po
    where = slice(half * HALF, half * HALF + HALF)
    cr = ci = None
    for mode in range(MODES):
        part = slice(mode * HALF, mode * HALF + HALF)
        nr = side_by_side(first[part, :HALF], second[part, :HALF])
        ni = side_by_side(first[part, HALF:], second[part, HALF:])
        pr, pi = probe[0, mode, where], probe[1, mode, where]
        tr = pr * nr + pi * ni
        ti = pr * ni - pi * nr
        cr = tr if cr is None else cr + tr
        ci = ti if ci is None else ci + ti
    block[0, where] = cr
    block[1, where] = ci


def rows_from(ref, start, count):
    group = lax.shift_right_arithmetic(start, 3)
    wide = ref[pl.ds(group, count // 8 + 1)].reshape(count + 8, SIDE)
    return pltpu.roll(wide, lax.rem(count + 8 - (start - group * 8), count + 8), 0)[:count]


def inside(value):
    return jnp.clip(value, 0, SIDE - 1)


def grouped(value):
    return value.reshape(value.shape[0] // 8, 8, SIDE)


def sort_amplitudes(amp, tabs, ratio):
    rest = amp[...]
    total = None
    for _ in range(3):
        piece = rest.astype(BF16)
        rest = rest - piece.astype(F32)
        moved = dot(dot(tabs[ORDER_T], piece).astype(BF16), tabs[ORDER])
        total = moved if total is None else total + moved
    ratio[0] = total[:HALF]
    ratio[1] = total[HALF:]


def sum_power(probe, padded, share):
    power = None
    for mode in range(MODES):
        term = probe[0, mode] * probe[0, mode] + probe[1, mode] * probe[1, mode]
        power = term if power is None else power + term
    padded[pl.ds(0, 32)] = jnp.zeros((32, 8, SIDE), F32)
    padded[pl.ds(32, 32)] = grouped(power)
    padded[pl.ds(64, 33)] = jnp.zeros((33, 8, SIDE), F32)
    share[...] = jnp.zeros_like(share)


def cut_patch(row_at, col_at, ext, patch):
    lanes = lax.broadcasted_iota(jnp.int32, (SIDE, SIDE), 1)
    back = lax.rem(SIDE - col_at, SIDE)
    for plane in range(2):
        here = pltpu.roll(rows_from(ext.at[0, plane], row_at, SIDE), back, 1)
        there = pltpu.roll(rows_from(ext.at[1, plane], row_at, SIDE), back, 1)
        patch[plane] = jnp.where(lanes < SIDE - col_at, here, there)


def make_ratio(far, ratio):
    for parity in range(2):
        seen = None
        for mode in range(MODES):
            re, im = far[mode, parity, :HALF], far[mode, parity, HALF:]
            term = re * re + im * im
            seen = term if seen is None else seen + term
        ratio[parity] = ratio[parity] / (jnp.sqrt(seen) + SOFTEN)


TOGETHER = 4


def add_spots(me, group, spots, padded, share):
    up, left = group // 2, group % 2
    known = jnp.logical_and(me.row >= up, me.col >= left)
    first = up * SIDE + me.z * QUART + SIDE
    row_base = (me.row - up) * SIDE
    col_base = (me.col - left) * SIDE
    lanes = lax.broadcasted_iota(jnp.int32, (QUART, SIDE), 1)

    def some(index, carry):
        total = share[...]
        for step in range(TOGETHER):
            spot = group * 16 + index * TOGETHER + step
            start = jnp.where(known, first - inside(spots[spot, 0, 0] - row_base), 0)
            turn = jnp.where(known, inside(spots[spot, 0, 1] - col_base), 0)
            turned = pltpu.roll(rows_from(padded, start, QUART), turn, 1)
            kept = lanes >= turn if left == 0 else lanes < turn
            total = total + jnp.where(kept, turned, 0.0)
        share[...] = total
        return carry

    lax.fori_loop(0, 16 // TOGETHER, some, 0)


def put_tall(value, col_at, tall):
    lanes = lax.broadcasted_iota(jnp.int32, (SIDE, SIDE), 1)
    turned = pltpu.roll(value, col_at, 1)
    tall[0, pl.ds(32, 32)] = grouped(jnp.where(lanes >= col_at, turned, 0.0))
    tall[1, pl.ds(32, 32)] = grouped(jnp.where(lanes < col_at, turned, 0.0))


def whole_kernel(
    offsets, obj_hbm, probe_hbm, amp_hbm, tabs_hbm, out,
    ext, spots, spot_words, probe, amp, tabs, patch, far, ratio, block, padded, share,
    twin_block, tall, low_sum, low_in, right_sum, right_in, total, z_in, x_out, x_in,
    load_sem,
    h_right_send, h_right_recv, h_low_send, h_low_recv, h_diag_send, h_diag_recv,
    h_pair_send, h_pair_recv, spot_send, spot_recv,
    pair_send, pair_recv, low_send, low_recv, right_send, right_recv,
    z_send, z_recv, x_send, x_recv, out_send, out_recv, twin_send, twin_recv,
):
    me = Place()
    core = me.core
    loads = [
        pltpu.make_async_copy(obj_hbm.at[0], ext.at[0, 0, pl.ds(0, SIDE // 8)], load_sem.at[0]),
        pltpu.make_async_copy(obj_hbm.at[1], ext.at[0, 1, pl.ds(0, SIDE // 8)], load_sem.at[1]),
        pltpu.make_async_copy(tabs_hbm, tabs, load_sem.at[2]),
        pltpu.make_async_copy(amp_hbm, amp, load_sem.at[3]),
        pltpu.make_async_copy(probe_hbm, probe, load_sem.at[4]),
    ]
    for load in loads:
        load.start()
    lanes = lax.broadcasted_iota(jnp.int32, (1, 1, 128), 2)
    line = jnp.where(lanes == 0, offsets[0, 0], jnp.where(lanes == 1, offsets[0, 1], 0))
    spots[pl.ds(me.layer, 1)] = line
    me.meet()
    loads[0].wait()
    loads[1].wait()

    def meanwhile():
        loads[2].wait()
        loads[3].wait()
        sort_amplitudes(amp, tabs, ratio)
        for source in range(2):
            for side in range(2):
                tall[source, side, pl.ds(0, 32)] = jnp.zeros((32, 8, SIDE), F32)
                tall[source, side, pl.ds(64, 33)] = jnp.zeros((33, 8, SIDE), F32)
        loads[4].wait()
        sum_power(probe, padded, share)

    halo(me, ext, spots, h_right_send, h_right_recv, h_low_send, h_low_recv, h_diag_send, h_diag_recv,
         h_pair_send, h_pair_recv, spot_send, spot_recv, meanwhile)
    words = pltpu.make_async_copy(spots, spot_words, load_sem.at[5])
    words.start()

    row_at = inside(offsets[0, 0] - me.row * SIDE)
    col_at = inside(offsets[0, 1] - me.col * SIDE)
    cut_patch(row_at, col_at, ext, patch)
    for mode in range(MODES):
        forward(mode, probe, patch, tabs, far)
    make_ratio(far, ratio)
    for mode in range(MODES):
        backward_rows(mode, ratio, tabs, far)
    words.wait()
    twin_layer = me.layer + 1 - 2 * core
    twin_row = inside(spot_words[twin_layer, 0, 0] - me.row * SIDE)
    twin_col = inside(spot_words[twin_layer, 0, 1] - me.col * SIDE)

    def pair_copy(half):
        where = pl.ds(half * HALF, HALF)
        return remote(block.at[1 - core, where], twin_block.at[where],
                      pair_send.at[half], pair_recv.at[half], me.partner)

    for half in range(2):
        backward_lanes(half, probe, tabs, far, block)
        pair_copy(half).start()

    has_right = me.col < 3
    has_left = me.col > 0
    top = me.row == 0
    bottom = me.row == 1
    parts = [(me.z + 1 + step) % 4 for step in range(4)]

    def low_copy(step):
        where = rows_of(parts[step])
        return remote(low_sum.at[:, where], low_in.at[:, where], low_send.at[step], low_recv.at[step], me.cross)

    def right_copy(step):
        where = rows_of(parts[step])
        return remote(right_sum.at[where], right_in.at[where], right_send.at[step], right_recv.at[step], me.right)

    def z_copy(step):
        return remote(total.at[rows_of(parts[step])], z_in.at[step], z_send.at[step], z_recv.at[step],
                      me.z_peer(step + 1))

    put_tall(block[core], col_at, tall.at[0])
    for half in range(2):
        pair_copy(half).wait_recv()
    put_tall(twin_block[...], twin_col, tall.at[1])

    def both(side, part, base):
        first = SIDE + base + part * QUART
        return (rows_from(tall.at[0, side], first - row_at, QUART)
                + rows_from(tall.at[1, side], first - twin_row, QUART))

    for step in range(4):
        where = rows_of(parts[step])

        @pl.when(top)
        def _():
            for side in range(2):
                low_sum[side, where] = both(side, parts[step], SIDE)
            low_copy(step).start()

        total[where] = both(0, parts[step], 0)
        right_sum[where] = both(1, parts[step], 0)

        @pl.when(bottom)
        def _():
            low_copy(step).wait_recv()
            total[where] = total[where] + low_in[0, where]
            right_sum[where] = right_sum[where] + low_in[1, where]

        @pl.when(has_right)
        def _():
            right_copy(step).start()

        add_spots(me, step, spot_words, padded, share)

    for step in range(4):
        where = rows_of(parts[step])

        @pl.when(has_left)
        def _():
            right_copy(step).wait_recv()
            total[where] = total[where] + right_in[where]

        if step < 3:
            z_copy(step).start()

    mine = rows_of(me.z)
    for step in range(3):
        z_copy(step).wait_recv()
    x_out[...] = total[mine] + z_in[0] + z_in[1] + z_in[2]
    x_copy = remote(x_out, x_in, x_send.at[0], x_recv.at[0], me.far_x)
    x_copy.start()
    x_copy.wait_recv()
    whole = x_out[...] + x_in[...]
    out[core, mine] = (whole + DAMPING * ext[0, core, groups_of(me.z)].reshape(QUART, SIDE)) / (share[...] + DAMPING)

    def out_copy(step):
        return remote(out.at[core, mine], out.at[core, mine], out_send.at[step], out_recv.at[step], me.z_peer(step + 1))

    def come_copy(step):
        where = out.at[core, rows_of((me.z + 3 - step) % 4)]
        return remote(where, where, out_send.at[step], out_recv.at[step], me.z_peer(step + 1))

    def twin_copy(step, plane):
        part = me.z if step == 3 else (me.z + 3 - step) % 4
        where = out.at[plane, rows_of(part)]
        return remote(where, where, twin_send.at[step], twin_recv.at[step], me.partner)

    for step in (1, 0, 2):
        out_copy(step).start()
    twin_copy(3, core).start()
    for step in (0, 2, 1):
        come_copy(step).wait_recv()
        twin_copy(step, core).start()
    for step in (3, 0, 2, 1):
        twin_copy(step, 1 - core).wait_recv()

    for half in range(2):
        pair_copy(half).wait_send()
    for step in range(4):
        twin_copy(step, core).wait_send()

        @pl.when(top)
        def _():
            low_copy(step).wait_send()

        @pl.when(has_right)
        def _():
            right_copy(step).wait_send()

        if step < 3:
            z_copy(step).wait_send()
            out_copy(step).wait_send()
    x_copy.wait_send()


def body(object_field, probe_modes, amplitudes, offsets):
    sems = pltpu.SemaphoreType.DMA
    return pl.pallas_call(
        whole_kernel,
        out_shape=jax.ShapeDtypeStruct((2, SIDE, SIDE), F32),
        in_specs=[SMEM_SPEC] + [ANY_SPEC] * 4,
        out_specs=VMEM_SPEC,
        scratch_shapes=[
            pltpu.VMEM((2, 2, 64, 8, SIDE), F32),
            pltpu.VMEM((64, 1, 128), jnp.int32),
            pltpu.SMEM((64, 1, 128), jnp.int32),
            pltpu.VMEM((2, MODES, SIDE, SIDE), F32),
            pltpu.VMEM((SIDE, SIDE), F32),
            pltpu.VMEM((10, SIDE, SIDE), BF16),
            pltpu.VMEM((2, SIDE, SIDE), F32),
            pltpu.VMEM((MODES, 2, SIDE, SIDE), F32),
            pltpu.VMEM((2, HALF, SIDE), F32),
            pltpu.VMEM((2, SIDE, SIDE), F32),
            pltpu.VMEM((97, 8, SIDE), F32),
            pltpu.VMEM((QUART, SIDE), F32),
            pltpu.VMEM((SIDE, SIDE), F32),
            pltpu.VMEM((2, 2, 97, 8, SIDE), F32),
            pltpu.VMEM((2, SIDE, SIDE), F32),
            pltpu.VMEM((2, SIDE, SIDE), F32),
            pltpu.VMEM((SIDE, SIDE), F32),
            pltpu.VMEM((SIDE, SIDE), F32),
            pltpu.VMEM((SIDE, SIDE), F32),
            pltpu.VMEM((3, QUART, SIDE), F32),
            pltpu.VMEM((QUART, SIDE), F32),
            pltpu.VMEM((QUART, SIDE), F32),
            sems((6,)),
            sems((4,)), sems((4,)), sems((4,)), sems((4,)), sems((4,)), sems((4,)),
            sems((3, 4)), sems((3, 4)), sems((7,)), sems((7,)),
            sems((2,)), sems((2,)), sems((4,)), sems((4,)), sems((4,)), sems((4,)),
            sems((3,)), sems((3,)), sems((1,)), sems((1,)), sems((3,)), sems((3,)), sems((4,)), sems((4,)),
        ],
        compiler_params=pltpu.CompilerParams(collective_id=0, has_side_effects=True),
        name="whole",
    )(offsets, object_field.reshape(2, 32, 8, SIDE), probe_modes, amplitudes[0], jnp.asarray(tables()))


def solution(mesh):
    placed = (
        P(None, "row", "col"),
        P(),
        P(("row", "col", "layer"), None, None),
        P(("row", "col", "layer"), None),
    )
    return jax.shard_map(
        body, mesh=mesh, in_specs=placed, out_specs=P(None, "row", "col"), check_vma=False
    )
```

time: 74.3 us -> 55.8 us (0.75)
  the two profiles are of different devices: /device:TPU:3 before, /device:TPU:11 now
where the time goes in v1:
time: 55.8 us; the launch traced here: 55.7 us
  Pallas kernels  53.8 us (96%)
  local copies, waits for them, and re-layouts  1.87 us (3%)
    pallas_call x1, Pallas kernels, body(): pl.pallas_call(whole_kernel, out_shape=jax.ShapeDtypeStruct((2, SIDE, SID...  53.8 us
    unnamed x1, local copies, waits for them, and re-layouts  1.87 us

profile of v1, /device:TPU:11, one launch (start us, length us, event | category | flops | bytes accessed | tf_op | source)
XLA Modules:
  0.0 55.7 jit_solution(15635254384612993724)
XLA Ops:
  0.0 53.8 %whole.1 = f32[2,256,256]{2,1,0:T(8,128)} custom-call(s32[1,2]{1,0:T(1,128)} %offsets.1, f32[2,32,8,256]{3,2,1,0:T(8,128)} %bitcast.2, f32[2,4,256,256]{3,2,1,0:T(8,128)} %probe_hbm.1, f32[256,256]{1,0:T(8,128)} %bitcast.3, bf16[10,256,256]{2,1,0:T(8,128)(2,1)} %constant.2.clone.tabs_hbm), custom_call_target="tpu_custom_call" | custom-call | tf_op jit(solution)/shard_map/whole/pallas_call | solution.py:602
  53.8 1.9 %copy.7 = f32[2,256,256]{2,1,0:T(8,128)} copy(f32[2,256,256]{2,1,0:T(8,128)} %whole.1) | data formatting | bytes 1048576

commit v2 on v1

--- a/solution.py
+++ b/solution.py
@@ -124,40 +124,160 @@
     return jnp.concatenate([upper, lower], axis=0)
 
 
-def halo(me, ext, spots, right_send, right_recv, low_send, low_recv, diag_send, diag_recv, pair_send, pair_recv,
-         spot_send, spot_recv, meanwhile):
+def halo(me, ext, right_send, right_recv, share_send, share_recv, low_send, low_recv, diag_send, diag_recv,
+         pair_send, pair_recv, meanwhile):
     core = me.core
     has_right = me.col < 3
     has_left = me.col > 0
     top = me.row == 0
     bottom = me.row == 1
 
-    def right_copy(part):
-        return remote(ext.at[0, core, groups_of(part)], ext.at[1, core, groups_of(part)],
-                      right_send.at[part], right_recv.at[part], me.left)
+    def piece(index, base=0):
+        if index == 0:
+            return pl.ds(base + me.z * 4, 4)
+        if index < 3:
+            return pl.ds(base + 8 + index * 8, 8)
+        return pl.ds(base + ((me.z + 6 - index) % 4) * 4, 4)
+
+    def right_copy(index):
+        return remote(ext.at[0, core, piece(index)], ext.at[1, core, piece(index)],
+                      right_send.at[index], right_recv.at[index], me.left)
+
+    def share_copy(step):
+        where = ext.at[1, core, piece(0)]
+        return remote(where, where, share_send.at[step - 1], share_recv.at[step - 1], me.z_peer(step))
 
     def low_copy(part):
         return remote(ext.at[0, core, groups_of(part)], ext.at[0, core, groups_of(part, SIDE)],
                       low_send.at[part], low_recv.at[part], me.cross)
 
-    def diag_copy(part):
-        return remote(ext.at[1, core, groups_of(part)], ext.at[1, core, groups_of(part, SIDE)],
-                      diag_send.at[part], diag_recv.at[part], me.cross)
-
-    def pair_copy(kind, part):
-        side, base = ((1, 0), (0, SIDE), (1, SIDE))[kind]
-        where = ext.at[side, core, groups_of(part, base)]
-        return remote(where, where, pair_send.at[kind, part], pair_recv.at[kind, part], me.partner)
+    def diag_copy(index):
+        return remote(ext.at[1, core, piece(index)], ext.at[1, core, piece(index, 32)],
+                      diag_send.at[index], diag_recv.at[index], me.cross)
+
+    def pair_copy(kind, index, plane):
+        if kind == 1:
+            where = ext.at[0, plane, groups_of(index, SIDE)]
+        else:
+            where = ext.at[1, plane, piece(index, 32 if kind == 2 else 0)]
+        sem = (0, 6, 10)[kind] + index
+        return remote(where, where, pair_send.at[sem], pair_recv.at[sem], me.partner)
 
     @pl.when(has_left)
     def _():
-        for part in range(4):
-            right_copy(part).start()
+        for index in range(3):
+            right_copy(index).start()
 
     @pl.when(bottom)
     def _():
         for part in range(4):
             low_copy(part).start()
+
+    meanwhile()
+
+    def pass_on(index):
+        @pl.when(bottom)
+        def _():
+            diag_copy(index).start()
+
+        pair_copy(0, index, core).start()
+
+    def low_here(part):
+        @pl.when(top)
+        def _():
+            low_copy(part).wait_recv()
+            pair_copy(1, part, core).start()
+
+    @pl.when(has_right)
+    def _():
+        right_copy(0).wait_recv()
+        for step in (2, 1, 3):
+            share_copy(step).start()
+        pass_on(0)
+
+    low_here(0)
+    low_here(1)
+
+    @pl.when(has_right)
+    def _():
+        right_copy(1).wait_recv()
+        pass_on(1)
+
+    low_here(2)
+    low_here(3)
+
+    @pl.when(has_right)
+    def _():
+        right_copy(2).wait_recv()
+        pass_on(2)
+        for step in (1, 3, 2):
+            share_copy(step).wait_recv()
+            pass_on(step + 2)
+
+    order = (0, 1, 2, 3, 5, 4)
+
+    @pl.when(jnp.logical_and(top, has_right))
+    def _():
+        for index in order:
+            diag_copy(index).wait_recv()
+            pair_copy(2, index, core).start()
+
+    @pl.when(has_right)
+    def _():
+        for index in order:
+            pair_copy(0, index, 1 - core).wait_recv()
+
+    @pl.when(top)
+    def _():
+        for part in range(4):
+            pair_copy(1, part, 1 - core).wait_recv()
+
+        @pl.when(has_right)
+        def _():
+            for index in order:
+                pair_copy(2, index, 1 - core).wait_recv()
+
+    def all_sent():
+        @pl.when(has_left)
+        def _():
+            for index in range(3):
+                right_copy(index).wait_send()
+
+        @pl.when(bottom)
+        def _():
+            for part in range(4):
+                low_copy(part).wait_send()
+
+            @pl.when(has_right)
+            def _():
+                for index in range(6):
+                    diag_copy(index).wait_send()
+
+        @pl.when(has_right)
+        def _():
+            for step in (1, 2, 3):
+                share_copy(step).wait_send()
+            for index in range(6):
+                pair_copy(0, index, core).wait_send()
+
+        @pl.when(top)
+        def _():
+            for part in range(4):
+                pair_copy(1, part, core).wait_send()
+
+            @pl.when(has_right)
+            def _():
+                for index in range(6):
+                    pair_copy(2, index, core).wait_send()
+
+    return all_sent
+
+
+def spot_chain(me, spots, spot_words, spot_send, spot_recv, word_sem):
+    has_right = me.col < 3
+    has_left = me.col > 0
+    top = me.row == 0
+    bottom = me.row == 1
 
     def spot_copy(step):
         if step == 0:
@@ -174,7 +294,10 @@
             return remote(spots.at[pl.ds(0, 16)], spots.at[pl.ds(16, 16)], spot_send.at[5], spot_recv.at[5], me.right)
         return remote(spots.at[pl.ds(0, 32)], spots.at[pl.ds(32, 32)], spot_send.at[6], spot_recv.at[6], me.cross)
 
-    def spots_go(stage):
+    near = pltpu.make_async_copy(spots.at[pl.ds(0, 16)], spot_words.at[pl.ds(0, 16)], word_sem.at[0])
+    others = pltpu.make_async_copy(spots.at[pl.ds(16, 48)], spot_words.at[pl.ds(16, 48)], word_sem.at[1])
+
+    def go(stage):
         if stage == 0:
             spot_copy(0).start()
         elif stage == 1:
@@ -187,6 +310,7 @@
         elif stage == 3:
             for step in (2, 3, 4):
                 spot_copy(step).wait_recv()
+            near.start()
 
             @pl.when(has_right)
             def _():
@@ -199,86 +323,25 @@
             @pl.when(top)
             def _():
                 spot_copy(6).start()
-        else:
+        elif stage == 5:
             @pl.when(bottom)
             def _():
                 spot_copy(6).wait_recv()
 
-    spots_go(0)
-    meanwhile()
-    for part in range(4):
-        @pl.when(has_right)
-        def _():
-            right_copy(part).wait_recv()
-
-            @pl.when(bottom)
-            def _():
-                diag_copy(part).start()
-
-            pair_copy(0, part).start()
-
-        @pl.when(top)
-        def _():
-            low_copy(part).wait_recv()
-            pair_copy(1, part).start()
-
-        spots_go(part + 1)
-
-    @pl.when(jnp.logical_and(top, has_right))
-    def _():
-        for part in range(4):
-            diag_copy(part).wait_recv()
-            pair_copy(2, part).start()
-
-    spots_go(5)
-
-    @pl.when(has_left)
-    def _():
-        for part in range(4):
-            right_copy(part).wait_send()
-
-    @pl.when(bottom)
-    def _():
-        for part in range(4):
-            low_copy(part).wait_send()
+            others.start()
+        else:
+            for step in range(5):
+                spot_copy(step).wait_send()
 
             @pl.when(has_right)
             def _():
-                diag_copy(part).wait_send()
-
-    @pl.when(has_right)
-    def _():
-        for part in range(4):
-            pair_copy(0, part).wait_send()
-            other_pair(ext, pair_send, pair_recv, me, 0, part).wait_recv()
-
-    @pl.when(top)
-    def _():
-        for part in range(4):
-            pair_copy(1, part).wait_send()
-            other_pair(ext, pair_send, pair_recv, me, 1, part).wait_recv()
-
-            @pl.when(has_right)
+                spot_copy(5).wait_send()
+
+            @pl.when(top)
             def _():
-                pair_copy(2, part).wait_send()
-                other_pair(ext, pair_send, pair_recv, me, 2, part).wait_recv()
-
-    for step in range(5):
-        spot_copy(step).wait_send()
-
-    @pl.when(has_right)
-    def _():
-        spot_copy(5).wait_send()
-
-    @pl.when(top)
-    def _():
-        spot_copy(6).wait_send()
-
-
-def other_pair(ext, pair_send, pair_recv, me, kind, part):
-    side, base = ((1, 0), (0, SIDE), (1, SIDE))[kind]
-    where = ext.at[side, 1 - me.core, groups_of(part, base)]
-    return remote(where, where, pair_send.at[kind, part], pair_recv.at[kind, part], me.partner)
+                spot_copy(6).wait_send()
+
+    return go, near, others
 
 
 def forward(mode, probe, patch, tabs, far):
@@ -422,8 +485,8 @@
     offsets, obj_hbm, probe_hbm, amp_hbm, tabs_hbm, out,
     ext, spots, spot_words, probe, amp, tabs, patch, far, ratio, block, padded, share,
     twin_block, tall, low_sum, low_in, right_sum, right_in, total, z_in, x_out, x_in,
-    load_sem,
-    h_right_send, h_right_recv, h_low_send, h_low_recv, h_diag_send, h_diag_recv,
+    load_sem, word_sem,
+    h_right_send, h_right_recv, h_share_send, h_share_recv, h_low_send, h_low_recv, h_diag_send, h_diag_recv,
     h_pair_send, h_pair_recv, spot_send, spot_recv,
     pair_send, pair_recv, low_send, low_recv, right_send, right_recv,
     z_send, z_recv, x_send, x_recv, out_send, out_recv, twin_send, twin_recv,
@@ -457,20 +520,24 @@
         loads[4].wait()
         sum_power(probe, padded, share)
 
-    halo(me, ext, spots, h_right_send, h_right_recv, h_low_send, h_low_recv, h_diag_send, h_diag_recv,
-         h_pair_send, h_pair_recv, spot_send, spot_recv, meanwhile)
-    words = pltpu.make_async_copy(spots, spot_words, load_sem.at[5])
-    words.start()
+    spots_go, near_words, other_words = spot_chain(me, spots, spot_words, spot_send, spot_recv, word_sem)
+    spots_go(0)
+    halo_sent = halo(me, ext, h_right_send, h_right_recv, h_share_send, h_share_recv, h_low_send, h_low_recv,
+                     h_diag_send, h_diag_recv, h_pair_send, h_pair_recv, meanwhile)
+    spots_go(1)
 
     row_at = inside(offsets[0, 0] - me.row * SIDE)
     col_at = inside(offsets[0, 1] - me.col * SIDE)
     cut_patch(row_at, col_at, ext, patch)
+    spots_go(2)
     for mode in range(MODES):
         forward(mode, probe, patch, tabs, far)
+    spots_go(3)
     make_ratio(far, ratio)
     for mode in range(MODES):
         backward_rows(mode, ratio, tabs, far)
-    words.wait()
+    spots_go(4)
+    near_words.wait()
     twin_layer = me.layer + 1 - 2 * core
     twin_row = inside(spot_words[twin_layer, 0, 0] - me.row * SIDE)
     twin_col = inside(spot_words[twin_layer, 0, 1] - me.col * SIDE)
@@ -483,6 +550,7 @@
     for half in range(2):
         backward_lanes(half, probe, tabs, far, block)
         pair_copy(half).start()
+    spots_go(5)
 
     has_right = me.col < 3
     has_left = me.col > 0
@@ -506,6 +574,7 @@
     for half in range(2):
         pair_copy(half).wait_recv()
     put_tall(twin_block[...], twin_col, tall.at[1])
+    other_words.wait()
 
     def both(side, part, base):
         first = SIDE + base + part * QUART
@@ -595,6 +664,8 @@
             z_copy(step).wait_send()
             out_copy(step).wait_send()
     x_copy.wait_send()
+    halo_sent()
+    spots_go(6)
 
 
 def body(object_field, probe_modes, amplitudes, offsets):
@@ -627,9 +698,9 @@
             pltpu.VMEM((3, QUART, SIDE), F32),
             pltpu.VMEM((QUART, SIDE), F32),
             pltpu.VMEM((QUART, SIDE), F32),
-            sems((6,)),
-            sems((4,)), sems((4,)), sems((4,)), sems((4,)), sems((4,)), sems((4,)),
-            sems((3, 4)), sems((3, 4)), sems((7,)), sems((7,)),
+            sems((5,)), sems((2,)),
+            sems((3,)), sems((3,)), sems((3,)), sems((3,)), sems((4,)), sems((4,)), sems((6,)), sems((6,)),
+            sems((16,)), sems((16,)), sems((7,)), sems((7,)),
             sems((2,)), sems((2,)), sems((4,)), sems((4,)), sems((4,)), sems((4,)),
             sems((3,)), sems((3,)), sems((1,)), sems((1,)), sems((3,)), sems((3,)), sems((4,)), sems((4,)),
         ],

time: 55.8 us -> 55.8 us (level)
  no operation moved by 1% of the time
where the time goes in v2:
time: 55.8 us; the launch traced here: 55.7 us
  Pallas kernels  53.8 us (96%)
  local copies, waits for them, and re-layouts  1.87 us (3%)
    pallas_call x1, Pallas kernels, body(): pl.pallas_call(whole_kernel, out_shape=jax.ShapeDtypeStruct((2, SIDE, SID...  53.8 us
    unnamed x1, local copies, waits for them, and re-layouts  1.87 us

profile of v2, /device:TPU:11, one launch (start us, length us, event | category | flops | bytes accessed | tf_op | source)
XLA Modules:
  0.0 55.7 jit_solution(5724950342991561051)
XLA Ops:
  0.0 53.8 %whole.1 = f32[2,256,256]{2,1,0:T(8,128)} custom-call(s32[1,2]{1,0:T(1,128)} %offsets.1, f32[2,32,8,256]{3,2,1,0:T(8,128)} %bitcast.2, f32[2,4,256,256]{3,2,1,0:T(8,128)} %probe_hbm.1, f32[256,256]{1,0:T(8,128)} %bitcast.3, bf16[10,256,256]{2,1,0:T(8,128)(2,1)} %constant.2.clone.tabs_hbm), custom_call_target="tpu_custom_call" | custom-call | tf_op jit(solution)/shard_map/whole/pallas_call | solution.py:673
  53.8 1.9 %copy.7 = f32[2,256,256]{2,1,0:T(8,128)} copy(f32[2,256,256]{2,1,0:T(8,128)} %whole.1) | data formatting | bytes 1048576

commit v3 on v2

--- a/solution.py
+++ b/solution.py
@@ -19,7 +19,7 @@
 BF16 = jnp.bfloat16
 VMEM_SPEC = pl.BlockSpec(memory_space=pltpu.VMEM)
 SMEM_SPEC = pl.BlockSpec(memory_space=pltpu.SMEM)
-ANY_SPEC = pl.BlockSpec(memory_space=pl.ANY)
+HBM_SPEC = pl.BlockSpec(memory_space=pltpu.HBM)
 
 
 def remote(src, dst, send, recv, device):
@@ -62,6 +62,7 @@
         barrier = pltpu.get_barrier_semaphore()
         others = [self.partner, self.far_x, self.cross, self.left, self.right]
         others += [self.z_peer(step) for step in (1, 2, 3)]
+        others += [self.at(z=(self.z + step) % 4, xh=1 - self.xh) for step in (1, 2, 3)]
         for other in others:
             pl.semaphore_signal(barrier, inc=1, device_id=other, device_id_type=pl.DeviceIdType.MESH)
         pl.semaphore_wait(barrier, len(others))
@@ -124,8 +125,13 @@
     return jnp.concatenate([upper, lower], axis=0)
 
 
+OWN = 5
+PIECES = 8
+ORDER_IN = (0, 1, 2, 5, 7, 3, 6, 4)
+
+
 def halo(me, ext, right_send, right_recv, share_send, share_recv, low_send, low_recv, diag_send, diag_recv,
-         pair_send, pair_recv, meanwhile):
+         pair_send, pair_recv, meanwhile, spots_go):
     core = me.core
     has_right = me.col < 3
     has_left = me.col > 0
@@ -134,10 +140,10 @@
 
     def piece(index, base=0):
         if index == 0:
-            return pl.ds(base + me.z * 4, 4)
-        if index < 3:
-            return pl.ds(base + 8 + index * 8, 8)
-        return pl.ds(base + ((me.z + 6 - index) % 4) * 4, 4)
+            return pl.ds(base + me.z * 2, 2)
+        if index < OWN:
+            return pl.ds(base + (0, 8, 16, 24, 28)[index], (0, 8, 8, 4, 4)[index])
+        return pl.ds(base + ((me.z + 3 + OWN - index) % 4) * 2, 2)
 
     def right_copy(index):
         return remote(ext.at[0, core, piece(index)], ext.at[1, core, piece(index)],
@@ -160,12 +166,12 @@
             where = ext.at[0, plane, groups_of(index, SIDE)]
         else:
             where = ext.at[1, plane, piece(index, 32 if kind == 2 else 0)]
-        sem = (0, 6, 10)[kind] + index
+        sem = (0, PIECES, PIECES + 4)[kind] + index
         return remote(where, where, pair_send.at[sem], pair_recv.at[sem], me.partner)
 
     @pl.when(has_left)
     def _():
-        for index in range(3):
+        for index in range(OWN):
             right_copy(index).start()
 
     @pl.when(bottom)
@@ -174,6 +180,7 @@
             low_copy(part).start()
 
     meanwhile()
+    spots_go(1)
 
     def pass_on(index):
         @pl.when(bottom)
@@ -203,28 +210,28 @@
         right_copy(1).wait_recv()
         pass_on(1)
 
+    spots_go(2)
     low_here(2)
     low_here(3)
 
     @pl.when(has_right)
     def _():
-        right_copy(2).wait_recv()
-        pass_on(2)
-        for step in (1, 3, 2):
-            share_copy(step).wait_recv()
-            pass_on(step + 2)
-
-    order = (0, 1, 2, 3, 5, 4)
+        for index in ORDER_IN[2:]:
+            if index < OWN:
+                right_copy(index).wait_recv()
+            else:
+                share_copy(index - OWN + 1).wait_recv()
+            pass_on(index)
 
     @pl.when(jnp.logical_and(top, has_right))
     def _():
-        for index in order:
+        for index in ORDER_IN:
             diag_copy(index).wait_recv()
             pair_copy(2, index, core).start()
 
     @pl.when(has_right)
     def _():
-        for index in order:
+        for index in ORDER_IN:
             pair_copy(0, index, 1 - core).wait_recv()
 
     @pl.when(top)
@@ -234,13 +241,13 @@
 
         @pl.when(has_right)
         def _():
-            for index in order:
+            for index in ORDER_IN:
                 pair_copy(2, index, 1 - core).wait_recv()
 
     def all_sent():
         @pl.when(has_left)
         def _():
-            for index in range(3):
+            for index in range(OWN):
                 right_copy(index).wait_send()
 
         @pl.when(bottom)
@@ -250,14 +257,14 @@
 
             @pl.when(has_right)
             def _():
-                for index in range(6):
+                for index in range(PIECES):
                     diag_copy(index).wait_send()
 
         @pl.when(has_right)
         def _():
             for step in (1, 2, 3):
                 share_copy(step).wait_send()
-            for index in range(6):
+            for index in range(PIECES):
                 pair_copy(0, index, core).wait_send()
 
         @pl.when(top)
@@ -267,7 +274,7 @@
 
             @pl.when(has_right)
             def _():
-                for index in range(6):
+                for index in range(PIECES):
                     pair_copy(2, index, core).wait_send()
 
     return all_sent
@@ -484,12 +491,12 @@
 def whole_kernel(
     offsets, obj_hbm, probe_hbm, amp_hbm, tabs_hbm, out,
     ext, spots, spot_words, probe, amp, tabs, patch, far, ratio, block, padded, share,
-    twin_block, tall, low_sum, low_in, right_sum, right_in, total, z_in, x_out, x_in,
+    twin_block, tall, low_sum, low_in, right_sum, right_in, total, z_in, far_in,
     load_sem, word_sem,
     h_right_send, h_right_recv, h_share_send, h_share_recv, h_low_send, h_low_recv, h_diag_send, h_diag_recv,
     h_pair_send, h_pair_recv, spot_send, spot_recv,
     pair_send, pair_recv, low_send, low_recv, right_send, right_recv,
-    z_send, z_recv, x_send, x_recv, out_send, out_recv, twin_send, twin_recv,
+    z_send, z_recv, far_send, far_recv, out_send, out_recv, twin_send, twin_recv,
 ):
     me = Place()
     core = me.core
@@ -523,20 +530,18 @@
     spots_go, near_words, other_words = spot_chain(me, spots, spot_words, spot_send, spot_recv, word_sem)
     spots_go(0)
     halo_sent = halo(me, ext, h_right_send, h_right_recv, h_share_send, h_share_recv, h_low_send, h_low_recv,
-                     h_diag_send, h_diag_recv, h_pair_send, h_pair_recv, meanwhile)
-    spots_go(1)
+                     h_diag_send, h_diag_recv, h_pair_send, h_pair_recv, meanwhile, spots_go)
+    spots_go(3)
 
     row_at = inside(offsets[0, 0] - me.row * SIDE)
     col_at = inside(offsets[0, 1] - me.col * SIDE)
     cut_patch(row_at, col_at, ext, patch)
-    spots_go(2)
     for mode in range(MODES):
         forward(mode, probe, patch, tabs, far)
-    spots_go(3)
+    spots_go(4)
     make_ratio(far, ratio)
     for mode in range(MODES):
         backward_rows(mode, ratio, tabs, far)
-    spots_go(4)
     near_words.wait()
     twin_layer = me.layer + 1 - 2 * core
     twin_row = inside(spot_words[twin_layer, 0, 0] - me.row * SIDE)
@@ -558,9 +563,10 @@
     bottom = me.row == 1
     parts = [(me.z + 1 + step) % 4 for step in range(4)]
 
-    def low_copy(step):
+    def low_copy(side, step):
         where = rows_of(parts[step])
-        return remote(low_sum.at[:, where], low_in.at[:, where], low_send.at[step], low_recv.at[step], me.cross)
+        return remote(low_sum.at[side, where], low_in.at[side, where],
+                      low_send.at[side, step], low_recv.at[side, step], me.cross)
 
     def right_copy(step):
         where = rows_of(parts[step])
@@ -569,6 +575,10 @@
     def z_copy(step):
         return remote(total.at[rows_of(parts[step])], z_in.at[step], z_send.at[step], z_recv.at[step],
                       me.z_peer(step + 1))
+
+    def far_copy(step):
+        return remote(total.at[rows_of(parts[step])], far_in.at[step], far_send.at[step], far_recv.at[step],
+                      me.at(z=parts[step], xh=1 - me.xh))
 
     put_tall(block[core], col_at, tall.at[0])
     for half in range(2):
@@ -581,33 +591,50 @@
         return (rows_from(tall.at[0, side], first - row_at, QUART)
                 + rows_from(tall.at[1, side], first - twin_row, QUART))
 
+    def send_low(side):
+        @pl.when(top)
+        def _():
+            for step in range(4):
+                low_sum[side, rows_of(parts[step])] = both(side, parts[step], SIDE)
+                low_copy(side, step).start()
+
+    send_low(1)
     for step in range(4):
         where = rows_of(parts[step])
-
-        @pl.when(top)
-        def _():
-            for side in range(2):
-                low_sum[side, where] = both(side, parts[step], SIDE)
-            low_copy(step).start()
-
-        total[where] = both(0, parts[step], 0)
         right_sum[where] = both(1, parts[step], 0)
 
-        @pl.when(bottom)
-        def _():
-            low_copy(step).wait_recv()
-            total[where] = total[where] + low_in[0, where]
+        @pl.when(jnp.logical_and(top, has_right))
+        def _():
+            right_copy(step).start()
+
+    send_low(0)
+    for step in range(4):
+        total[rows_of(parts[step])] = both(0, parts[step], 0)
+    for group in range(2):
+        add_spots(me, group, spot_words, padded, share)
+
+    @pl.when(bottom)
+    def _():
+        for step in range(4):
+            where = rows_of(parts[step])
+            low_copy(1, step).wait_recv()
             right_sum[where] = right_sum[where] + low_in[1, where]
 
-        @pl.when(has_right)
-        def _():
-            right_copy(step).start()
-
-        add_spots(me, step, spot_words, padded, share)
+            @pl.when(has_right)
+            def _():
+                right_copy(step).start()
+
+    for group in range(2, 4):
+        add_spots(me, group, spot_words, padded, share)
 
     for step in range(4):
         where = rows_of(parts[step])
 
+        @pl.when(bottom)
+        def _():
+            low_copy(0, step).wait_recv()
+            total[where] = total[where] + low_in[0, where]
+
         @pl.when(has_left)
         def _():
             right_copy(step).wait_recv()
@@ -615,15 +642,16 @@
 
         if step < 3:
             z_copy(step).start()
+        far_copy(step).start()
 
     mine = rows_of(me.z)
     for step in range(3):
         z_copy(step).wait_recv()
-    x_out[...] = total[mine] + z_in[0] + z_in[1] + z_in[2]
-    x_copy = remote(x_out, x_in, x_send.at[0], x_recv.at[0], me.far_x)
-    x_copy.start()
-    x_copy.wait_recv()
-    whole = x_out[...] + x_in[...]
+    near_sum = total[mine] + z_in[0] + z_in[1] + z_in[2]
+    for step in range(4):
+        far_copy(step).wait_recv()
+    far_sum = far_in[3] + far_in[0] + far_in[1] + far_in[2]
+    whole = near_sum + far_sum
     out[core, mine] = (whole + DAMPING * ext[0, core, groups_of(me.z)].reshape(QUART, SIDE)) / (share[...] + DAMPING)
 
     def out_copy(step):
@@ -652,9 +680,12 @@
     for step in range(4):
         twin_copy(step, core).wait_send()
 
+        far_copy(step).wait_send()
+
         @pl.when(top)
         def _():
-            low_copy(step).wait_send()
+            for side in range(2):
+                low_copy(side, step).wait_send()
 
         @pl.when(has_right)
         def _():
@@ -663,7 +694,6 @@
         if step < 3:
             z_copy(step).wait_send()
             out_copy(step).wait_send()
-    x_copy.wait_send()
     halo_sent()
     spots_go(6)
 
@@ -672,8 +702,8 @@
     sems = pltpu.SemaphoreType.DMA
     return pl.pallas_call(
         whole_kernel,
-        out_shape=jax.ShapeDtypeStruct((2, SIDE, SIDE), F32),
-        in_specs=[SMEM_SPEC] + [ANY_SPEC] * 4,
+        out_shape=pltpu.VMEM((2, SIDE, SIDE), F32),
+        in_specs=[SMEM_SPEC] + [HBM_SPEC] * 4,
         out_specs=VMEM_SPEC,
         scratch_shapes=[
             pltpu.VMEM((2, 2, 64, 8, SIDE), F32),
@@ -696,15 +726,16 @@
             pltpu.VMEM((SIDE, SIDE), F32),
             pltpu.VMEM((SIDE, SIDE), F32),
             pltpu.VMEM((3, QUART, SIDE), F32),
-            pltpu.VMEM((QUART, SIDE), F32),
-            pltpu.VMEM((QUART, SIDE), F32),
+            pltpu.VMEM((4, QUART, SIDE), F32),
             sems((5,)), sems((2,)),
-            sems((3,)), sems((3,)), sems((3,)), sems((3,)), sems((4,)), sems((4,)), sems((6,)), sems((6,)),
-            sems((16,)), sems((16,)), sems((7,)), sems((7,)),
-            sems((2,)), sems((2,)), sems((4,)), sems((4,)), sems((4,)), sems((4,)),
-            sems((3,)), sems((3,)), sems((1,)), sems((1,)), sems((3,)), sems((3,)), sems((4,)), sems((4,)),
+            sems((OWN,)), sems((OWN,)), sems((3,)), sems((3,)), sems((4,)), sems((4,)),
+            sems((PIECES,)), sems((PIECES,)), sems((2 * PIECES + 4,)), sems((2 * PIECES + 4,)), sems((7,)), sems((7,)),
+            sems((2,)), sems((2,)), sems((2, 4)), sems((2, 4)), sems((4,)), sems((4,)),
+            sems((3,)), sems((3,)), sems((4,)), sems((4,)), sems((3,)), sems((3,)), sems((4,)), sems((4,)),
         ],
-        compiler_params=pltpu.CompilerParams(collective_id=0, has_side_effects=True),
+        compiler_params=pltpu.CompilerParams(
+            collective_id=0, has_side_effects=True
+        ),
         name="whole",
     )(offsets, object_field.reshape(2, 32, 8, SIDE), probe_modes, amplitudes[0], jnp.asarray(tables()))
 

time: 55.8 us -> 50 us (0.90)
  the two profiles are of different devices: /device:TPU:11 before, /device:TPU:1 now
where the time goes in v3:
time: 50 us; the launch traced here: 49.9 us
  Pallas kernels  49.1 us (98%)
  local copies, waits for them, and re-layouts  0.8 us (2%)
    pallas_call x1, Pallas kernels, body(): pl.pallas_call(whole_kernel, out_shape=pltpu.VMEM((2, SIDE, SIDE), F32),...  49.1 us

profile of v3, /device:TPU:1, one launch (start us, length us, event | category | flops | bytes accessed | tf_op | source)
XLA Modules:
  0.0 49.9 jit_solution(13473857598024893124)
XLA Ops:
  0.0 49.1 %whole.1 = f32[2,256,256]{2,1,0:T(8,128)S(1)} custom-call(s32[1,2]{1,0:T(1,128)} %offsets.1, f32[2,32,8,256]{3,2,1,0:T(8,128)} %bitcast.2, f32[2,4,256,256]{3,2,1,0:T(8,128)} %probe_hbm.1, f32[256,256]{1,0:T(8,128)} %bitcast.3, bf16[10,256,256]{2,1,0:T(8,128)(2,1)} %constant.2.clone.tabs_hbm), custom_call_target="tpu_custom_call" | custom-call | tf_op jit(solution)/shard_map/whole/pallas_call | solution.py:703
  49.1 0.8 %copy.7 = f32[2,256,256]{2,1,0:T(8,128)} copy(f32[2,256,256]{2,1,0:T(8,128)S(1)} %whole.1) | data formatting | bytes 1048576

commit v4 on v3

--- a/solution.py
+++ b/solution.py
@@ -62,7 +62,6 @@
         barrier = pltpu.get_barrier_semaphore()
         others = [self.partner, self.far_x, self.cross, self.left, self.right]
         others += [self.z_peer(step) for step in (1, 2, 3)]
-        others += [self.at(z=(self.z + step) % 4, xh=1 - self.xh) for step in (1, 2, 3)]
         for other in others:
             pl.semaphore_signal(barrier, inc=1, device_id=other, device_id_type=pl.DeviceIdType.MESH)
         pl.semaphore_wait(barrier, len(others))
@@ -126,8 +125,8 @@
 
 
 OWN = 5
-PIECES = 8
-ORDER_IN = (0, 1, 2, 5, 7, 3, 6, 4)
+PIECES = 6
+ORDER_IN = (0, 1, 2, 3, 4, 5)
 
 
 def halo(me, ext, right_send, right_recv, share_send, share_recv, low_send, low_recv, diag_send, diag_recv,
@@ -138,20 +137,23 @@
     top = me.row == 0
     bottom = me.row == 1
 
+    odd = me.z % 2
+    z_mate = me.at(z=me.z + 1 - 2 * odd)
+
     def piece(index, base=0):
         if index == 0:
-            return pl.ds(base + me.z * 2, 2)
+            return pl.ds(base + odd * 6, 6)
         if index < OWN:
-            return pl.ds(base + (0, 8, 16, 24, 28)[index], (0, 8, 8, 4, 4)[index])
-        return pl.ds(base + ((me.z + 3 + OWN - index) % 4) * 2, 2)
+            return pl.ds(base + (0, 12, 20, 26, 30)[index], (0, 8, 6, 4, 2)[index])
+        return pl.ds(base + (1 - odd) * 6, 6)
 
     def right_copy(index):
         return remote(ext.at[0, core, piece(index)], ext.at[1, core, piece(index)],
                       right_send.at[index], right_recv.at[index], me.left)
 
-    def share_copy(step):
+    def share_copy():
         where = ext.at[1, core, piece(0)]
-        return remote(where, where, share_send.at[step - 1], share_recv.at[step - 1], me.z_peer(step))
+        return remote(where, where, share_send.at[0], share_recv.at[0], z_mate)
 
     def low_copy(part):
         return remote(ext.at[0, core, groups_of(part)], ext.at[0, core, groups_of(part, SIDE)],
@@ -198,8 +200,7 @@
     @pl.when(has_right)
     def _():
         right_copy(0).wait_recv()
-        for step in (2, 1, 3):
-            share_copy(step).start()
+        share_copy().start()
         pass_on(0)
 
     low_here(0)
@@ -220,7 +221,7 @@
             if index < OWN:
                 right_copy(index).wait_recv()
             else:
-                share_copy(index - OWN + 1).wait_recv()
+                share_copy().wait_recv()
             pass_on(index)
 
     @pl.when(jnp.logical_and(top, has_right))
@@ -262,8 +263,7 @@
 
         @pl.when(has_right)
         def _():
-            for step in (1, 2, 3):
-                share_copy(step).wait_send()
+            share_copy().wait_send()
             for index in range(PIECES):
                 pair_copy(0, index, core).wait_send()
 
@@ -728,7 +728,7 @@
             pltpu.VMEM((3, QUART, SIDE), F32),
             pltpu.VMEM((4, QUART, SIDE), F32),
             sems((5,)), sems((2,)),
-            sems((OWN,)), sems((OWN,)), sems((3,)), sems((3,)), sems((4,)), sems((4,)),
+            sems((OWN,)), sems((OWN,)), sems((1,)), sems((1,)), sems((4,)), sems((4,)),
             sems((PIECES,)), sems((PIECES,)), sems((2 * PIECES + 4,)), sems((2 * PIECES + 4,)), sems((7,)), sems((7,)),
             sems((2,)), sems((2,)), sems((2, 4)), sems((2, 4)), sems((4,)), sems((4,)),
             sems((3,)), sems((3,)), sems((4,)), sems((4,)), sems((3,)), sems((3,)), sems((4,)), sems((4,)),

time: 50 us -> 49.2 us (0.984)
  Pallas kernels: 49.1 us -> 48.3 us
    pallas_call x1, Pallas kernels: 49.1 us -> 48.3 us  [body(): pl.pallas_call(whole_kernel, out_shape=pltpu.VMEM((2, SIDE, SIDE), F32),...]
where the time goes in v4:
time: 49.2 us; the launch traced here: 49.1 us
  Pallas kernels  48.3 us (98%)
  local copies, waits for them, and re-layouts  0.8 us (2%)
    pallas_call x1, Pallas kernels, body(): pl.pallas_call(whole_kernel, out_shape=pltpu.VMEM((2, SIDE, SIDE), F32),...  48.3 us

profile of v4, /device:TPU:1, one launch (start us, length us, event | category | flops | bytes accessed | tf_op | source)
XLA Modules:
  0.0 49.1 jit_solution(14438311941064552781)
XLA Ops:
  0.0 48.3 %whole.1 = f32[2,256,256]{2,1,0:T(8,128)S(1)} custom-call(s32[1,2]{1,0:T(1,128)} %offsets.1, f32[2,32,8,256]{3,2,1,0:T(8,128)} %bitcast.2, f32[2,4,256,256]{3,2,1,0:T(8,128)} %probe_hbm.1, f32[256,256]{1,0:T(8,128)} %bitcast.3, bf16[10,256,256]{2,1,0:T(8,128)(2,1)} %constant.2.clone.tabs_hbm), custom_call_target="tpu_custom_call" | custom-call | tf_op jit(solution)/shard_map/whole/pallas_call | solution.py:703
  48.3 0.8 %copy.7 = f32[2,256,256]{2,1,0:T(8,128)} copy(f32[2,256,256]{2,1,0:T(8,128)S(1)} %whole.1) | data formatting | bytes 1048576

commit v5 on v4

--- a/solution.py
+++ b/solution.py
@@ -15,6 +15,7 @@
 SIDE = 256
 HALF = 128
 QUART = 64
+EIGHTH = 32
 F32 = jnp.float32
 BF16 = jnp.bfloat16
 VMEM_SPEC = pl.BlockSpec(memory_space=pltpu.VMEM)
@@ -44,6 +45,7 @@
         self.core = layer % 2
         self.partner = self.at(xh=self.xh, core=1 - self.core)
         self.far_x = self.at(xh=1 - self.xh)
+        self.far_twin = self.at(xh=1 - self.xh, core=1 - self.core)
         self.cross_xh = (self.xh + self.core) % 2
         self.cross = {"row": 1 - self.row, "layer": self.z * 4 + self.cross_xh * 2 + self.core}
         self.left = {"col": (self.col + 3) % 4}
@@ -60,7 +62,7 @@
 
     def meet(self):
         barrier = pltpu.get_barrier_semaphore()
-        others = [self.partner, self.far_x, self.cross, self.left, self.right]
+        others = [self.partner, self.far_x, self.far_twin, self.cross, self.left, self.right]
         others += [self.z_peer(step) for step in (1, 2, 3)]
         for other in others:
             pl.semaphore_signal(barrier, inc=1, device_id=other, device_id_type=pl.DeviceIdType.MESH)
@@ -182,7 +184,6 @@
             low_copy(part).start()
 
     meanwhile()
-    spots_go(1)
 
     def pass_on(index):
         @pl.when(bottom)
@@ -287,12 +288,10 @@
     bottom = me.row == 1
 
     def spot_copy(step):
-        if step == 0:
+        if step in (0, 1, 7):
             where = pl.ds(me.layer, 1)
-            return remote(spots.at[where], spots.at[where], spot_send.at[0], spot_recv.at[0], me.partner)
-        if step == 1:
-            where = pl.ds(me.z * 4 + me.xh * 2, 2)
-            return remote(spots.at[where], spots.at[where], spot_send.at[1], spot_recv.at[1], me.far_x)
+            other = {0: me.partner, 1: me.far_x, 7: me.far_twin}[step]
+            return remote(spots.at[where], spots.at[where], spot_send.at[step], spot_recv.at[step], other)
         if step < 5:
             where = pl.ds(me.z * 4, 4)
             return remote(spots.at[where], spots.at[where], spot_send.at[step], spot_recv.at[step],
@@ -306,12 +305,11 @@
 
     def go(stage):
         if stage == 0:
-            spot_copy(0).start()
-        elif stage == 1:
-            spot_copy(0).wait_recv()
-            spot_copy(1).start()
+            for step in (1, 7, 0):
+                spot_copy(step).start()
         elif stage == 2:
-            spot_copy(1).wait_recv()
+            for step in (0, 1, 7):
+                spot_copy(step).wait_recv()
             for step in (2, 3, 4):
                 spot_copy(step).start()
         elif stage == 3:
@@ -337,7 +335,7 @@
 
             others.start()
         else:
-            for step in range(5):
+            for step in (0, 1, 2, 3, 4, 7):
                 spot_copy(step).wait_send()
 
             @pl.when(has_right)
@@ -555,7 +553,6 @@
     for half in range(2):
         backward_lanes(half, probe, tabs, far, block)
         pair_copy(half).start()
-    spots_go(5)
 
     has_right = me.col < 3
     has_left = me.col > 0
@@ -563,60 +560,65 @@
     bottom = me.row == 1
     parts = [(me.z + 1 + step) % 4 for step in range(4)]
 
+    def rows_at(step):
+        return pl.ds(pl.multiple_of(parts[step // 2] * QUART + step % 2 * EIGHTH, EIGHTH), EIGHTH)
+
     def low_copy(side, step):
-        where = rows_of(parts[step])
+        where = rows_at(step) if side == 1 else rows_of(parts[step])
         return remote(low_sum.at[side, where], low_in.at[side, where],
                       low_send.at[side, step], low_recv.at[side, step], me.cross)
 
     def right_copy(step):
-        where = rows_of(parts[step])
+        where = rows_at(step)
         return remote(right_sum.at[where], right_in.at[where], right_send.at[step], right_recv.at[step], me.right)
 
     def z_copy(step):
-        return remote(total.at[rows_of(parts[step])], z_in.at[step], z_send.at[step], z_recv.at[step],
-                      me.z_peer(step + 1))
+        return remote(total.at[rows_at(step)], z_in.at[step], z_send.at[step], z_recv.at[step],
+                      me.z_peer(step // 2 + 1))
 
     def far_copy(step):
-        return remote(total.at[rows_of(parts[step])], far_in.at[step], far_send.at[step], far_recv.at[step],
-                      me.at(z=parts[step], xh=1 - me.xh))
+        return remote(total.at[rows_at(step)], far_in.at[step], far_send.at[step], far_recv.at[step],
+                      me.at(z=parts[step // 2], xh=1 - me.xh))
 
     put_tall(block[core], col_at, tall.at[0])
     for half in range(2):
         pair_copy(half).wait_recv()
     put_tall(twin_block[...], twin_col, tall.at[1])
-    other_words.wait()
-
-    def both(side, part, base):
-        first = SIDE + base + part * QUART
-        return (rows_from(tall.at[0, side], first - row_at, QUART)
-                + rows_from(tall.at[1, side], first - twin_row, QUART))
-
-    def send_low(side):
-        @pl.when(top)
-        def _():
-            for step in range(4):
-                low_sum[side, rows_of(parts[step])] = both(side, parts[step], SIDE)
-                low_copy(side, step).start()
-
-    send_low(1)
+
+    def both(side, first, count):
+        return (rows_from(tall.at[0, side], SIDE + first - row_at, count)
+                + rows_from(tall.at[1, side], SIDE + first - twin_row, count))
+
+    def first_of(step):
+        return parts[step // 2] * QUART + step % 2 * EIGHTH
+
+    @pl.when(top)
+    def _():
+        for step in range(8):
+            low_sum[1, rows_at(step)] = both(1, SIDE + first_of(step), EIGHTH)
+            low_copy(1, step).start()
+
+    for step in range(8):
+        right_sum[rows_at(step)] = both(1, first_of(step), EIGHTH)
+
+        @pl.when(jnp.logical_and(top, has_right))
+        def _():
+            right_copy(step).start()
+
+    @pl.when(top)
+    def _():
+        for step in range(4):
+            low_sum[0, rows_of(parts[step])] = both(0, SIDE + parts[step] * QUART, QUART)
+            low_copy(0, step).start()
+
     for step in range(4):
-        where = rows_of(parts[step])
-        right_sum[where] = both(1, parts[step], 0)
-
-        @pl.when(jnp.logical_and(top, has_right))
-        def _():
-            right_copy(step).start()
-
-    send_low(0)
-    for step in range(4):
-        total[rows_of(parts[step])] = both(0, parts[step], 0)
-    for group in range(2):
-        add_spots(me, group, spot_words, padded, share)
+        total[rows_of(parts[step])] = both(0, parts[step] * QUART, QUART)
+    add_spots(me, 0, spot_words, padded, share)
 
     @pl.when(bottom)
     def _():
-        for step in range(4):
-            where = rows_of(parts[step])
+        for step in range(8):
+            where = rows_at(step)
             low_copy(1, step).wait_recv()
             right_sum[where] = right_sum[where] + low_in[1, where]
 
@@ -624,76 +626,88 @@
             def _():
                 right_copy(step).start()
 
-    for group in range(2, 4):
+    spots_go(5)
+    other_words.wait()
+    for group in range(1, 4):
         add_spots(me, group, spot_words, padded, share)
 
-    for step in range(4):
-        where = rows_of(parts[step])
-
-        @pl.when(bottom)
-        def _():
-            low_copy(0, step).wait_recv()
-            total[where] = total[where] + low_in[0, where]
+    for step in range(8):
+        where = rows_at(step)
+        if step % 2 == 0:
+            @pl.when(bottom)
+            def _():
+                low_copy(0, step // 2).wait_recv()
+                lower = rows_of(parts[step // 2])
+                total[lower] = total[lower] + low_in[0, lower]
 
         @pl.when(has_left)
         def _():
             right_copy(step).wait_recv()
             total[where] = total[where] + right_in[where]
 
-        if step < 3:
+        far_copy(step).start()
+        if step < 6:
             z_copy(step).start()
-        far_copy(step).start()
-
-    mine = rows_of(me.z)
-    for step in range(3):
-        z_copy(step).wait_recv()
-    near_sum = total[mine] + z_in[0] + z_in[1] + z_in[2]
-    for step in range(4):
-        far_copy(step).wait_recv()
-    far_sum = far_in[3] + far_in[0] + far_in[1] + far_in[2]
-    whole = near_sum + far_sum
-    out[core, mine] = (whole + DAMPING * ext[0, core, groups_of(me.z)].reshape(QUART, SIDE)) / (share[...] + DAMPING)
-
-    def out_copy(step):
-        return remote(out.at[core, mine], out.at[core, mine], out_send.at[step], out_recv.at[step], me.z_peer(step + 1))
-
-    def come_copy(step):
-        where = out.at[core, rows_of((me.z + 3 - step) % 4)]
-        return remote(where, where, out_send.at[step], out_recv.at[step], me.z_peer(step + 1))
-
-    def twin_copy(step, plane):
+
+    def out_rows(part, half):
+        return pl.ds(pl.multiple_of(part * QUART + half * EIGHTH, EIGHTH), EIGHTH)
+
+    def out_copy(step, half):
+        where = out.at[core, out_rows(me.z, half)]
+        return remote(where, where, out_send.at[step, half], out_recv.at[step, half], me.z_peer(step + 1))
+
+    def come_copy(step, half):
+        where = out.at[core, out_rows((me.z + 3 - step) % 4, half)]
+        return remote(where, where, out_send.at[step, half], out_recv.at[step, half], me.z_peer(step + 1))
+
+    def twin_copy(step, half, plane):
         part = me.z if step == 3 else (me.z + 3 - step) % 4
-        where = out.at[plane, rows_of(part)]
-        return remote(where, where, twin_send.at[step], twin_recv.at[step], me.partner)
-
-    for step in (1, 0, 2):
-        out_copy(step).start()
-    twin_copy(3, core).start()
-    for step in (0, 2, 1):
-        come_copy(step).wait_recv()
-        twin_copy(step, core).start()
-    for step in (3, 0, 2, 1):
-        twin_copy(step, 1 - core).wait_recv()
+        where = out.at[plane, out_rows(part, half)]
+        return remote(where, where, twin_send.at[step, half], twin_recv.at[step, half], me.partner)
+
+    for half in range(2):
+        mine = out_rows(me.z, half)
+        for step in range(3):
+            z_copy(2 * step + half).wait_recv()
+        near_sum = total[mine] + z_in[half] + z_in[2 + half] + z_in[4 + half]
+        for step in range(4):
+            far_copy(2 * step + half).wait_recv()
+        far_sum = far_in[6 + half] + far_in[half] + far_in[2 + half] + far_in[4 + half]
+        own = ext[0, core, pl.ds(me.z * 8 + half * 4, 4)].reshape(EIGHTH, SIDE)
+        below = share[half * EIGHTH : half * EIGHTH + EIGHTH] + DAMPING
+        out[core, mine] = (near_sum + far_sum + DAMPING * own) / below
+        for step in (1, 0, 2):
+            out_copy(step, half).start()
+        twin_copy(3, half, core).start()
+
+    for half in range(2):
+        for step in (0, 2, 1):
+            come_copy(step, half).wait_recv()
+            twin_copy(step, half, core).start()
+    for half in range(2):
+        for step in (3, 0, 2, 1):
+            twin_copy(step, half, 1 - core).wait_recv()
 
     for half in range(2):
         pair_copy(half).wait_send()
-    for step in range(4):
-        twin_copy(step, core).wait_send()
-
+        for step in range(4):
+            twin_copy(step, half, core).wait_send()
+            if step < 3:
+                out_copy(step, half).wait_send()
+    for step in range(8):
         far_copy(step).wait_send()
+        if step < 6:
+            z_copy(step).wait_send()
 
         @pl.when(top)
         def _():
-            for side in range(2):
-                low_copy(side, step).wait_send()
+            low_copy(1, step).wait_send()
+            if step < 4:
+                low_copy(0, step).wait_send()
 
         @pl.when(has_right)
         def _():
             right_copy(step).wait_send()
-
-        if step < 3:
-            z_copy(step).wait_send()
-            out_copy(step).wait_send()
     halo_sent()
     spots_go(6)
 
@@ -725,13 +739,13 @@
             pltpu.VMEM((SIDE, SIDE), F32),
             pltpu.VMEM((SIDE, SIDE), F32),
             pltpu.VMEM((SIDE, SIDE), F32),
-            pltpu.VMEM((3, QUART, SIDE), F32),
-            pltpu.VMEM((4, QUART, SIDE), F32),
+            pltpu.VMEM((6, EIGHTH, SIDE), F32),
+            pltpu.VMEM((8, EIGHTH, SIDE), F32),
             sems((5,)), sems((2,)),
             sems((OWN,)), sems((OWN,)), sems((1,)), sems((1,)), sems((4,)), sems((4,)),
-            sems((PIECES,)), sems((PIECES,)), sems((2 * PIECES + 4,)), sems((2 * PIECES + 4,)), sems((7,)), sems((7,)),
-            sems((2,)), sems((2,)), sems((2, 4)), sems((2, 4)), sems((4,)), sems((4,)),
-            sems((3,)), sems((3,)), sems((4,)), sems((4,)), sems((3,)), sems((3,)), sems((4,)), sems((4,)),
+            sems((PIECES,)), sems((PIECES,)), sems((2 * PIECES + 4,)), sems((2 * PIECES + 4,)), sems((8,)), sems((8,)),
+            sems((2,)), sems((2,)), sems((2, 8)), sems((2, 8)), sems((8,)), sems((8,)),
+            sems((6,)), sems((6,)), sems((8,)), sems((8,)), sems((3, 2)), sems((3, 2)), sems((4, 2)), sems((4, 2)),
         ],
         compiler_params=pltpu.CompilerParams(
             collective_id=0, has_side_effects=True

time: 49.2 us -> 48.7 us (0.990)
  Pallas kernels: 48.3 us -> 47.8 us
where the time goes in v5:
time: 48.7 us; the launch traced here: 48.6 us
  Pallas kernels  47.8 us (98%)
  local copies, waits for them, and re-layouts  0.8 us (2%)
    pallas_call x1, Pallas kernels, body(): pl.pallas_call(whole_kernel, out_shape=pltpu.VMEM((2, SIDE, SIDE), F32),...  47.8 us

profile of v5, /device:TPU:1, one launch (start us, length us, event | category | flops | bytes accessed | tf_op | source)
XLA Modules:
  0.0 48.6 jit_solution(9776341806997713964)
XLA Ops:
  0.0 47.8 %whole.1 = f32[2,256,256]{2,1,0:T(8,128)S(1)} custom-call(s32[1,2]{1,0:T(1,128)} %offsets.1, f32[2,32,8,256]{3,2,1,0:T(8,128)} %bitcast.2, f32[2,4,256,256]{3,2,1,0:T(8,128)} %probe_hbm.1, f32[256,256]{1,0:T(8,128)} %bitcast.3, bf16[10,256,256]{2,1,0:T(8,128)(2,1)} %constant.2.clone.tabs_hbm), custom_call_target="tpu_custom_call" | custom-call | tf_op jit(solution)/shard_map/whole/pallas_call | solution.py:717
  47.8 0.8 %copy.7 = f32[2,256,256]{2,1,0:T(8,128)} copy(f32[2,256,256]{2,1,0:T(8,128)S(1)} %whole.1) | data formatting | bytes 1048576

commit v6 on v5

--- a/solution.py
+++ b/solution.py
@@ -459,10 +459,10 @@
 def add_spots(me, group, spots, padded, share):
     up, left = group // 2, group % 2
     known = jnp.logical_and(me.row >= up, me.col >= left)
-    first = up * SIDE + me.z * QUART + SIDE
+    first = up * SIDE + me.z * QUART + me.xh * EIGHTH + SIDE
     row_base = (me.row - up) * SIDE
     col_base = (me.col - left) * SIDE
-    lanes = lax.broadcasted_iota(jnp.int32, (QUART, SIDE), 1)
+    lanes = lax.broadcasted_iota(jnp.int32, (EIGHTH, SIDE), 1)
 
     def some(index, carry):
         total = share[...]
@@ -470,7 +470,7 @@
             spot = group * 16 + index * TOGETHER + step
             start = jnp.where(known, first - inside(spots[spot, 0, 0] - row_base), 0)
             turn = jnp.where(known, inside(spots[spot, 0, 1] - col_base), 0)
-            turned = pltpu.roll(rows_from(padded, start, QUART), turn, 1)
+            turned = pltpu.roll(rows_from(padded, start, EIGHTH), turn, 1)
             kept = lanes >= turn if left == 0 else lanes < turn
             total = total + jnp.where(kept, turned, 0.0)
         share[...] = total
@@ -560,8 +560,11 @@
     bottom = me.row == 1
     parts = [(me.z + 1 + step) % 4 for step in range(4)]
 
+    def unit(part, half):
+        return pl.ds(pl.multiple_of(part * QUART + half * EIGHTH, EIGHTH), EIGHTH)
+
     def rows_at(step):
-        return pl.ds(pl.multiple_of(parts[step // 2] * QUART + step % 2 * EIGHTH, EIGHTH), EIGHTH)
+        return unit(parts[step // 2], step % 2)
 
     def low_copy(side, step):
         where = rows_at(step) if side == 1 else rows_of(parts[step])
@@ -573,12 +576,12 @@
         return remote(right_sum.at[where], right_in.at[where], right_send.at[step], right_recv.at[step], me.right)
 
     def z_copy(step):
-        return remote(total.at[rows_at(step)], z_in.at[step], z_send.at[step], z_recv.at[step],
-                      me.z_peer(step // 2 + 1))
+        return remote(total.at[unit(parts[step], me.xh)], z_in.at[step], z_send.at[step], z_recv.at[step],
+                      me.z_peer(step + 1))
 
     def far_copy(step):
-        return remote(total.at[rows_at(step)], far_in.at[step], far_send.at[step], far_recv.at[step],
-                      me.at(z=parts[step // 2], xh=1 - me.xh))
+        return remote(total.at[unit(parts[step], 1 - me.xh)], far_in.at[step], far_send.at[step], far_recv.at[step],
+                      me.at(z=parts[step], xh=1 - me.xh))
 
     put_tall(block[core], col_at, tall.at[0])
     for half in range(2):
@@ -645,58 +648,58 @@
             right_copy(step).wait_recv()
             total[where] = total[where] + right_in[where]
 
-        far_copy(step).start()
+        @pl.when(me.xh != step % 2)
+        def _():
+            far_copy(step // 2).start()
+
         if step < 6:
-            z_copy(step).start()
-
-    def out_rows(part, half):
-        return pl.ds(pl.multiple_of(part * QUART + half * EIGHTH, EIGHTH), EIGHTH)
-
-    def out_copy(step, half):
-        where = out.at[core, out_rows(me.z, half)]
-        return remote(where, where, out_send.at[step, half], out_recv.at[step, half], me.z_peer(step + 1))
-
-    def come_copy(step, half):
-        where = out.at[core, out_rows((me.z + 3 - step) % 4, half)]
-        return remote(where, where, out_send.at[step, half], out_recv.at[step, half], me.z_peer(step + 1))
-
-    def twin_copy(step, half, plane):
-        part = me.z if step == 3 else (me.z + 3 - step) % 4
-        where = out.at[plane, out_rows(part, half)]
-        return remote(where, where, twin_send.at[step, half], twin_recv.at[step, half], me.partner)
-
-    for half in range(2):
-        mine = out_rows(me.z, half)
-        for step in range(3):
-            z_copy(2 * step + half).wait_recv()
-        near_sum = total[mine] + z_in[half] + z_in[2 + half] + z_in[4 + half]
-        for step in range(4):
-            far_copy(2 * step + half).wait_recv()
-        far_sum = far_in[6 + half] + far_in[half] + far_in[2 + half] + far_in[4 + half]
-        own = ext[0, core, pl.ds(me.z * 8 + half * 4, 4)].reshape(EIGHTH, SIDE)
-        below = share[half * EIGHTH : half * EIGHTH + EIGHTH] + DAMPING
-        out[core, mine] = (near_sum + far_sum + DAMPING * own) / below
-        for step in (1, 0, 2):
-            out_copy(step, half).start()
-        twin_copy(3, half, core).start()
-
-    for half in range(2):
-        for step in (0, 2, 1):
-            come_copy(step, half).wait_recv()
-            twin_copy(step, half, core).start()
-    for half in range(2):
-        for step in (3, 0, 2, 1):
-            twin_copy(step, half, 1 - core).wait_recv()
+            @pl.when(me.xh == step % 2)
+            def _():
+                z_copy(step // 2).start()
+
+    def out_copy(index):
+        where = out.at[core, unit(me.z, me.xh)]
+        there = me.z_peer(index + 1) if index < 3 else me.at(z=(me.z + index - 3) % 4, xh=1 - me.xh)
+        return remote(where, where, out_send.at[index], out_recv.at[index], there)
+
+    def unit_of(index):
+        if index < 3:
+            return unit((me.z + 3 - index) % 4, me.xh)
+        if index < 7:
+            return unit((me.z + 7 - index) % 4, 1 - me.xh)
+        return unit(me.z, me.xh)
+
+    def twin_copy(index, plane):
+        where = out.at[plane, unit_of(index)]
+        return remote(where, where, twin_send.at[index], twin_recv.at[index], me.partner)
+
+    mine = unit(me.z, me.xh)
+    for step in range(3):
+        z_copy(step).wait_recv()
+    near_sum = total[mine] + z_in[0] + z_in[1] + z_in[2]
+    for step in range(4):
+        far_copy(step).wait_recv()
+    far_sum = far_in[3] + far_in[0] + far_in[1] + far_in[2]
+    own = ext[0, core, pl.ds(me.z * 8 + me.xh * 4, 4)].reshape(EIGHTH, SIDE)
+    out[core, mine] = (near_sum + far_sum + DAMPING * own) / (share[...] + DAMPING)
+    for index in (5, 4, 6, 3, 1, 0, 2):
+        out_copy(index).start()
+    twin_copy(7, core).start()
+    for index in (0, 2, 1, 3, 4, 6, 5):
+        out_copy(index).wait_recv()
+        twin_copy(index, core).start()
+    for index in (7, 0, 2, 1, 3, 4, 6, 5):
+        twin_copy(index, 1 - core).wait_recv()
 
     for half in range(2):
         pair_copy(half).wait_send()
-        for step in range(4):
-            twin_copy(step, half, core).wait_send()
-            if step < 3:
-                out_copy(step, half).wait_send()
     for step in range(8):
-        far_copy(step).wait_send()
-        if step < 6:
+        twin_copy(step, core).wait_send()
+        if step < 7:
+            out_copy(step).wait_send()
+        if step < 4:
+            far_copy(step).wait_send()
+        if step < 3:
             z_copy(step).wait_send()
 
         @pl.when(top)
@@ -731,7 +734,7 @@
             pltpu.VMEM((2, HALF, SIDE), F32),
             pltpu.VMEM((2, SIDE, SIDE), F32),
             pltpu.VMEM((97, 8, SIDE), F32),
-            pltpu.VMEM((QUART, SIDE), F32),
+            pltpu.VMEM((EIGHTH, SIDE), F32),
             pltpu.VMEM((SIDE, SIDE), F32),
             pltpu.VMEM((2, 2, 97, 8, SIDE), F32),
             pltpu.VMEM((2, SIDE, SIDE), F32),
@@ -739,13 +742,13 @@
             pltpu.VMEM((SIDE, SIDE), F32),
             pltpu.VMEM((SIDE, SIDE), F32),
             pltpu.VMEM((SIDE, SIDE), F32),
-            pltpu.VMEM((6, EIGHTH, SIDE), F32),
-            pltpu.VMEM((8, EIGHTH, SIDE), F32),
+            pltpu.VMEM((3, EIGHTH, SIDE), F32),
+            pltpu.VMEM((4, EIGHTH, SIDE), F32),
             sems((5,)), sems((2,)),
             sems((OWN,)), sems((OWN,)), sems((1,)), sems((1,)), sems((4,)), sems((4,)),
             sems((PIECES,)), sems((PIECES,)), sems((2 * PIECES + 4,)), sems((2 * PIECES + 4,)), sems((8,)), sems((8,)),
             sems((2,)), sems((2,)), sems((2, 8)), sems((2, 8)), sems((8,)), sems((8,)),
-            sems((6,)), sems((6,)), sems((8,)), sems((8,)), sems((3, 2)), sems((3, 2)), sems((4, 2)), sems((4, 2)),
+            sems((3,)), sems((3,)), sems((4,)), sems((4,)), sems((7,)), sems((7,)), sems((8,)), sems((8,)),
         ],
         compiler_params=pltpu.CompilerParams(
             collective_id=0, has_side_effects=True

time: 48.7 us -> 47.4 us (0.973)
  Pallas kernels: 47.8 us -> 46.5 us
    pallas_call x1, Pallas kernels: 47.8 us -> 46.5 us  [body(): pl.pallas_call(whole_kernel, out_shape=pltpu.VMEM((2, SIDE, SIDE), F32),...]
where the time goes in v6:
time: 47.4 us; the launch traced here: 47.3 us
  Pallas kernels  46.5 us (98%)
  local copies, waits for them, and re-layouts  0.8 us (2%)
    pallas_call x1, Pallas kernels, body(): pl.pallas_call(whole_kernel, out_shape=pltpu.VMEM((2, SIDE, SIDE), F32),...  46.5 us

profile of v6, /device:TPU:1, one launch (start us, length us, event | category | flops | bytes accessed | tf_op | source)
XLA Modules:
  0.0 47.3 jit_solution(7506630950523746470)
XLA Ops:
  0.0 46.5 %whole.1 = f32[2,256,256]{2,1,0:T(8,128)S(1)} custom-call(s32[1,2]{1,0:T(1,128)} %offsets.1, f32[2,32,8,256]{3,2,1,0:T(8,128)} %bitcast.2, f32[2,4,256,256]{3,2,1,0:T(8,128)} %probe_hbm.1, f32[256,256]{1,0:T(8,128)} %bitcast.3, bf16[10,256,256]{2,1,0:T(8,128)(2,1)} %constant.2.clone.tabs_hbm), custom_call_target="tpu_custom_call" | custom-call | tf_op jit(solution)/shard_map/whole/pallas_call | solution.py:720
  46.5 0.8 %copy.7 = f32[2,256,256]{2,1,0:T(8,128)} copy(f32[2,256,256]{2,1,0:T(8,128)S(1)} %whole.1) | data formatting | bytes 1048576

commit v7 on v6

--- a/solution.py
+++ b/solution.py
@@ -144,10 +144,10 @@
 
     def piece(index, base=0):
         if index == 0:
-            return pl.ds(base + odd * 6, 6)
+            return pl.ds(base + odd * 5, 5)
         if index < OWN:
-            return pl.ds(base + (0, 12, 20, 26, 30)[index], (0, 8, 6, 4, 2)[index])
-        return pl.ds(base + (1 - odd) * 6, 6)
+            return pl.ds(base + (0, 10, 18, 25, 29)[index], (0, 8, 7, 4, 3)[index])
+        return pl.ds(base + (1 - odd) * 5, 5)
 
     def right_copy(index):
         return remote(ext.at[0, core, piece(index)], ext.at[1, core, piece(index)],
@@ -529,15 +529,15 @@
     spots_go(0)
     halo_sent = halo(me, ext, h_right_send, h_right_recv, h_share_send, h_share_recv, h_low_send, h_low_recv,
                      h_diag_send, h_diag_recv, h_pair_send, h_pair_recv, meanwhile, spots_go)
-    spots_go(3)
 
     row_at = inside(offsets[0, 0] - me.row * SIDE)
     col_at = inside(offsets[0, 1] - me.col * SIDE)
     cut_patch(row_at, col_at, ext, patch)
     for mode in range(MODES):
         forward(mode, probe, patch, tabs, far)
+    spots_go(3)
+    make_ratio(far, ratio)
     spots_go(4)
-    make_ratio(far, ratio)
     for mode in range(MODES):
         backward_rows(mode, ratio, tabs, far)
     near_words.wait()
@@ -558,7 +558,7 @@
     has_left = me.col > 0
     top = me.row == 0
     bottom = me.row == 1
-    parts = [(me.z + 1 + step) % 4 for step in range(4)]
+    parts = [(me.z + step) % 4 for step in (2, 1, 3, 0)]
 
     def unit(part, half):
         return pl.ds(pl.multiple_of(part * QUART + half * EIGHTH, EIGHTH), EIGHTH)
@@ -577,7 +577,7 @@
 
     def z_copy(step):
         return remote(total.at[unit(parts[step], me.xh)], z_in.at[step], z_send.at[step], z_recv.at[step],
-                      me.z_peer(step + 1))
+                      me.at(z=parts[step]))
 
     def far_copy(step):
         return remote(total.at[unit(parts[step], 1 - me.xh)], far_in.at[step], far_send.at[step], far_recv.at[step],

time: 47.4 us -> 47.6 us (level)
  no operation moved by 1% of the time
where the time goes in v7:
time: 47.6 us; the launch traced here: 47.3 us
  Pallas kernels  46.5 us (98%)
  local copies, waits for them, and re-layouts  0.8 us (2%)
    pallas_call x1, Pallas kernels, body(): pl.pallas_call(whole_kernel, out_shape=pltpu.VMEM((2, SIDE, SIDE), F32),...  46.5 us

profile of v7, /device:TPU:1, one launch (start us, length us, event | category | flops | bytes accessed | tf_op | source)
XLA Modules:
  0.0 47.3 jit_solution(2162385897018478885)
XLA Ops:
  0.0 46.5 %whole.1 = f32[2,256,256]{2,1,0:T(8,128)S(1)} custom-call(s32[1,2]{1,0:T(1,128)} %offsets.1, f32[2,32,8,256]{3,2,1,0:T(8,128)} %bitcast.2, f32[2,4,256,256]{3,2,1,0:T(8,128)} %probe_hbm.1, f32[256,256]{1,0:T(8,128)} %bitcast.3, bf16[10,256,256]{2,1,0:T(8,128)(2,1)} %constant.2.clone.tabs_hbm), custom_call_target="tpu_custom_call" | custom-call | tf_op jit(solution)/shard_map/whole/pallas_call | solution.py:720
  46.5 0.8 %copy.7 = f32[2,256,256]{2,1,0:T(8,128)} copy(f32[2,256,256]{2,1,0:T(8,128)S(1)} %whole.1) | data formatting | bytes 1048576
